TPU v7x, 256 devices: a whole 4x4x8 slice. The times are simulated.
256 devices in a mesh: field: 16 (over y_hi, z), gx: 4 (over x), gy: 4 (over y_lo, core).
Axes of the slice: x: 4, y: 4 (y_hi: 2, y_lo: 2; y = y_hi * 2 + y_lo), z: 8, core: 2. Of those that a mesh axis runs over, the one named last changes fastest.
Arguments:
- concentrations: float32 [16, 16, 16, 32, 128], P('field', None, 'gx', 'gy'), may hold values from 0 to 2
- velocity: float32 [3, 16, 32, 128], P(None, 'gx', 'gy'), may hold values from -0.3 to 0.3
- diffusivity: float32 [16, 32, 128], P('gx', 'gy'), may hold values from 0.02 to 0.12
- wiener: float32 [2, 3, 16, 16, 32, 128], P(None, None, 'field', 'gx', 'gy'), may hold values from -1.8 to 1.8
- mix_rate: float32 [16, 32, 128], P('gx', 'gy'), may hold values from 0.2 to 2
- rate_constants: float32 [64], replicated, may hold values from 0.1 to 1
- reactions: int32 [64, 4], replicated, may hold values from 0 to 15
Outputs:
- advanced: float32 [16, 16, 16, 32, 128], P('field', None, 'gx', 'gy')
Inputs may be any that keep to these rules, and one draw needn't show every extreme that they name: `reactions`: each row names two reactant and two product scalars.
All inputs are finite; a program needn't handle non-finite values.
Results may differ from a plain program's by a relative error of at most 0.0001.
Values sent between devices are 32-bit elements; how exact they have to be, the bound alone decides.
A program may use at most 64 MiB of HBM per device.

v0:
```python
import jax
import jax.numpy as jnp
from jax import lax
from jax.sharding import PartitionSpec as P

SUBSTEPS = 12
STEPS = 2


chem_step = 0.04
highest = lax.Precision.HIGHEST


def padded_2(value, sides, width):
    edges = {}
    for axis, dim in sides:
        devices, length = (lax.axis_size(axis), value.shape[dim])
        up = [(i, (i + 1) % devices) for i in range(devices - 1)]
        last = lax.slice_in_dim(value, length - width, length, axis=dim)
        initial = lax.slice_in_dim(value, 0, width, axis=dim)
        edges[dim] = (
            lax.ppermute(last, axis, up),
            lax.ppermute(initial, axis, [(b, a) for a, b in up]),
        )
    done = []
    for _, dim in sides:
        low, high = edges[dim]
        around = [(width, width) if d in done else (0, 0) for d in range(value.ndim)]
        value = jnp.concatenate([jnp.pad(low, around), value, jnp.pad(high, around)], axis=dim)
        done.append(dim)
    return value


def cut_along(value, dim, devices):
    lengths = value.shape
    tiles = value.reshape(*lengths[:dim], devices, lengths[dim] // devices, *lengths[dim + 1 :])
    return jnp.moveaxis(tiles, dim, 0)


def sum_at_owner(value, axis, dim):
    tiles = cut_along(value, dim, lax.axis_size(axis))
    arrived = lax.all_to_all(tiles, axis, split_axis=0, concat_axis=0, tiled=True)
    return arrived.sum(axis=0)


def side_by_side(arrays, axis, dim, along):
    ends, at = ([], 0)
    for a in arrays[:-1]:
        at += a.shape[along]
        ends.append(at)
    both = jnp.concatenate(arrays, axis=along)
    return tuple(jnp.split(sum_at_owner(both, axis, dim), ends, axis=along))


def copy_for_each(value, axis):
    copies = jnp.broadcast_to(value, (lax.axis_size(axis), *value.shape))
    return lax.all_to_all(copies, axis, split_axis=0, concat_axis=0, tiled=True)


def joined_along(tiles, dim):
    tiles = jnp.moveaxis(tiles, 0, dim)
    lengths = tiles.shape
    return tiles.reshape(*lengths[:dim], lengths[dim] * lengths[dim + 1], *lengths[dim + 2 :])


def gather_directly(value, axis, dim):
    tiles = copy_for_each(value, axis)
    return joined_along(tiles, dim)


def tables(reactions, count):
    scalar_ids = jnp.arange(count, dtype=jnp.int32)[None, :]
    react = (reactions[:, 0:1] == scalar_ids).astype(jnp.float32) + (
        reactions[:, 1:2] == scalar_ids
    ).astype(jnp.float32)
    produce = (reactions[:, 2:3] == scalar_ids).astype(jnp.float32) + (
        reactions[:, 3:4] == scalar_ids
    ).astype(jnp.float32)
    return (react, (produce - react).T)


def neighbours(values):
    middle = (slice(1, -1), slice(1, -1), slice(1, -1))
    leading = (slice(None),) * (values.ndim - 3)
    result = []
    for dim_index in range(3):
        upper_cut = list(middle)
        upper_cut[dim_index] = slice(2, None)
        lower_cut = list(middle)
        lower_cut[dim_index] = slice(0, -2)
        result.append((values[leading + tuple(upper_cut)], values[leading + tuple(lower_cut)]))
    return result


def transport(padded, gamma_pad, gamma, velocity, increments):
    centre = padded[:, 1:-1, 1:-1, 1:-1]
    pairs = neighbours(padded)
    gamma_pairs = neighbours(gamma_pad)
    noise_amp = jnp.sqrt(2.0 * gamma)
    change = jnp.zeros_like(centre)
    for dim_index in range(3):
        upward, downward = pairs[dim_index]
        gamma_up, gamma_down = gamma_pairs[dim_index]
        change = (
            change
            + 0.5 * (gamma + gamma_up) * (upward - centre)
            + 0.5 * (gamma + gamma_down) * (downward - centre)
        )
        change = change + (noise_amp * increments[dim_index] - velocity[dim_index]) * (
            0.5 * (upward - downward)
        )
    return centre + change


def chemistry(values, react, net_t, rate_constants):

    def substep(index, conc):
        logs = jnp.log(jax.nn.softplus(conc))
        flux = rate_constants[:, None] * jnp.exp(jnp.dot(react, logs, precision=highest))
        return conc + chem_step * jnp.dot(net_t, flux, precision=highest)

    return lax.fori_loop(0, SUBSTEPS, substep, values)


def closure(first, second, count, mix_rate):
    mean = first / count
    meansq = second / count
    spread = jnp.sum(meansq - mean * mean, axis=0)
    energy = jnp.sum(meansq, axis=0)
    omega = mix_rate * (1.0 + spread / (1.0 + energy))
    return (mean, jnp.exp(-0.5 * omega))


def on_device(concentrations, velocity, diffusivity, wiener, mix_rate, rate_constants, reactions):
    conc = concentrations[0]
    scalars = conc.shape[0]
    react, net_t = tables(reactions, scalars)
    count = lax.axis_size("field")
    gamma_rim = padded_2(diffusivity, (("gx", 0), ("gy", 1)), 1)
    gamma_pad = jnp.pad(gamma_rim, ((0, 0), (0, 0), (1, 1)))
    for step_index in range(STEPS):
        rimmed = padded_2(conc, (("gx", 1), ("gy", 2)), 1)
        padded = jnp.pad(rimmed, ((0, 0), (0, 0), (0, 0), (1, 1)))
        moved = transport(padded, gamma_pad, diffusivity, velocity, wiener[step_index, :, 0])
        conc = chemistry(moved.reshape(scalars, -1), react, net_t, rate_constants).reshape(
            moved.shape
        )
        cell_rows = conc.shape[1] * conc.shape[2]
        depth = conc.shape[3]
        flat_conc = conc.reshape(scalars, cell_rows, depth)
        first, second = side_by_side((flat_conc, flat_conc * flat_conc), "field", 1, 0)
        share_len = first.shape[1]
        start = lax.axis_index("field") * share_len
        rate_share = lax.dynamic_slice_in_dim(
            mix_rate.reshape(cell_rows, depth), start, share_len, 0
        )
        mean_share, decay_share = closure(first, second, count, rate_share)
        mean_flat, decay_flat = (
            gather_directly(mean_share, "field", 1),
            gather_directly(decay_share, "field", 0),
        )
        mean = mean_flat.reshape(conc.shape)
        decay = decay_flat.reshape(conc.shape[1:])
        conc = mean + (conc - mean) * decay
    return conc[None]


def solution(mesh):
    return jax.shard_map(
        on_device,
        mesh=mesh,
        in_specs=(
            P("field", None, "gx", "gy", None),
            P(None, "gx", "gy", None),
            P("gx", "gy", None),
            P(None, None, "field", "gx", "gy", None),
            P("gx", "gy", None),
            P(),
            P(),
        ),
        out_specs=P("field", None, "gx", "gy", None),
        check_vma=False,
    )
```

profile of v0, /device:TPU:4, one launch (start us, length us, event | category | flops | bytes accessed | tf_op | source)
XLA Modules:
  0.0 199.3 jit_solution(599475773969795769)
XLA Ops:
  0.0 1.1 copy.43
  1.1 2.4 %collective-permute-start.1 = (f32[16,1,8,128]{3,0,2,1:T(8,128)S(1)}, f32[16,1,8,128]{3,0,2,1:T(8,128)S(1)}, u32[]{:S(2)}, u32[]{:S(2)}) collective-permute-start(f32[16,1,8,128]{3,0,2,1:T(8,128)S(1)} %get-tuple-element.195), channel_id=1, source_target_pairs={{4,0},{8,4},{12,8},{5,1},{9,5},{13,9},{6,2},{10,6},{14,10},{7,3},{... | collective-permute-start | bytes 196616 | tf_op jit(solution)/shard_map/ppermute | solution.py:23
  3.6 3.4 %collective-permute-start.3 = (f32[16,1,8,128]{3,0,2,1:T(8,128)S(1)}, f32[16,1,8,128]{3,0,2,1:T(8,128)S(1)}, u32[]{:S(2)}, u32[]{:S(2)}) collective-permute-start(f32[16,1,8,128]{3,0,2,1:T(8,128)S(1)} %get-tuple-element.196), channel_id=1, source_target_pairs={{0,4},{4,8},{8,12},{1,5},{5,9},{9,13},{2,6},{6,10},{10,14},{3,7},{... | collective-permute-start | bytes 196616 | tf_op jit(solution)/shard_map/ppermute | solution.py:22
  7.0 1.9 collective-permute-start.2
  9.0 1.3 collective-permute-start.4
  10.3 3.0 %collective-permute-start.6 = (f32[4,1,128]{2,1,0:T(1,128)S(1)}, f32[4,1,128]{2,1,0:T(1,128)S(1)}, u32[]{:S(2)}, u32[]{:S(2)}) collective-permute-start(f32[4,1,128]{2,1,0:T(1,128)S(1)} %get-tuple-element.214), channel_id=1, source_target_pairs={{0,1},{1,2},{2,3},{4,5},{5,6},{6,7},{8,9},{9,10},{10,11},{12,13},{... | collective-permute-start | bytes 6152 | tf_op jit(solution)/shard_map/ppermute | solution.py:22
  13.4 1.3 collective-permute-start.5
  14.7 3.7 %collective-permute-start.7 = (f32[16,4,1,128]{3,0,2,1:T(8,128)S(1)}, f32[16,4,1,128]{3,0,2,1:T(8,128)S(1)}, u32[]{:S(2)}, u32[]{:S(2)}) collective-permute-start(f32[16,4,1,128]{3,0,2,1:T(8,128)S(1)} %get-tuple-element.193), channel_id=1, source_target_pairs={{0,1},{1,2},{2,3},{4,5},{5,6},{6,7},{8,9},{9,10},{10,11},{12,13},{... | collective-permute-start | bytes 98312 | tf_op jit(solution)/shard_map/ppermute | solution.py:22
  18.5 4.1 %collective-permute-start = (f32[1,8,128]{2,1,0:T(8,128)S(1)}, f32[1,8,128]{2,1,0:T(8,128)S(1)}, u32[]{:S(2)}, u32[]{:S(2)}) collective-permute-start(f32[1,8,128]{2,1,0:T(8,128)S(1)} %get-tuple-element.216), channel_id=1, source_target_pairs={{4,0},{8,4},{12,8},{5,1},{9,5},{13,9},{6,2},{10,6},{14,10},{7,3},{... | collective-permute-start | bytes 12296 | tf_op jit(solution)/shard_map/ppermute | solution.py:23
  22.5 1.6 collective-permute-done
  26.6 21.8 %while.24 = (s32[]{:T(128)}, f32[16,4096]{1,0:T(8,128)S(1)}, f32[64]{0:T(128)S(1)}, s32[64]{0:T(128)S(1)}, s32[64]{0:T(128)S(1)}, /*index=5*/s32[64]{0:T(128)S(1)}, s32[64]{0:T(128)S(1)}, s32[]{:T(128)}) while((s32[]{:T(128)}, f32[16,4096]{1,0:T(8,128)S(1)}, f32[64]{0:T(128)S(1)}, s32[64]{0:T(128)S(1)}, ...), condition=%wide.region_1.2_spmd.clone.clone, body=%wide.region_0.1_spmd.clone.clone.sunk | while | flops 101466112 | bytes 2885461 | solution.py:122
  28.4 1.1 fusion.147
  30.3 1.1 fusion.147
  32.1 1.1 fusion.147
  33.9 1.1 fusion.147
  35.7 1.1 fusion.147
  37.5 1.1 fusion.147
  39.3 1.1 fusion.147
  41.1 1.1 fusion.147
  43.0 1.1 fusion.147
  44.8 1.1 fusion.147
  46.6 1.1 fusion.147
  49.3 28.3 %all_to_all.30 = f32[16,32,2,128]{3,2,1,0:T(2,128)S(1)} all-to-all(f32[16,32,2,128]{3,2,1,0:T(2,128)S(1)} %copy.16), channel_id=1, replica_groups=mesh['field'=16,'gx'=4,'gy'=4] {'field'}, dimensions={0} | all-to-all | bytes 1048576 | tf_op jit(solution)/shard_map/all_to_all | solution.py:42
  78.6 4.9 %all-to-all-start.1 = ((f32[16,16,2,128]{3,2,1,0:T(2,128)}), f32[16,16,2,128]{3,2,1,0:T(2,128)S(1)}, u32[]{:S(2)}, u32[]{:S(2)}) async-start(f32[16,16,2,128]{3,2,1,0:T(2,128)} %broadcast_in_dim.8), calls=%async_computation.1 | async-start | bytes 524288 | tf_op jit(solution)/shard_map/all_to_all | solution.py:57
  84.3 11.1 %all-to-all-done.1 = f32[16,16,2,128]{3,2,1,0:T(2,128)S(1)} async-done(((f32[16,16,2,128]{3,2,1,0:T(2,128)}), f32[16,16,2,128]{3,2,1,0:T(2,128)S(1)}, u32[]{:S(2)}, u32[]{:S(2)}) %all-to-all-start.1) | async-done | bytes 262176 | tf_op jit(solution)/shard_map/all_to_all | solution.py:57
  95.9 4.5 %all-to-all-start.2 = ((f32[16,2,128]{2,1,0:T(2,128)}), f32[16,2,128]{2,1,0:T(2,128)S(1)}, u32[]{:S(2)}, u32[]{:S(2)}) async-start(f32[16,2,128]{2,1,0:T(2,128)} %broadcast_in_dim.9), calls=%async_computation.2 | async-start | bytes 32768 | tf_op jit(solution)/shard_map/all_to_all | solution.py:57
  100.6 9.9 %all-to-all-done.2 = f32[16,2,128]{2,1,0:T(2,128)S(1)} async-done(((f32[16,2,128]{2,1,0:T(2,128)}), f32[16,2,128]{2,1,0:T(2,128)S(1)}, u32[]{:S(2)}, u32[]{:S(2)}) %all-to-all-start.2) | async-done | bytes 16416 | tf_op jit(solution)/shard_map/all_to_all | solution.py:57
  110.7 3.9 %collective-permute-start.8 = (f32[16,1,8,128]{3,0,2,1:T(8,128)S(1)}, f32[16,1,8,128]{3,0,2,1:T(8,128)S(1)}, u32[]{:S(2)}, u32[]{:S(2)}) collective-permute-start(f32[16,1,8,128]{3,0,2,1:T(8,128)S(1)} %get-tuple-element.191), channel_id=1, source_target_pairs={{4,0},{8,4},{12,8},{5,1},{9,5},{13,9},{6,2},{10,6},{14,10},{7,3},{... | collective-permute-start | bytes 196616 | tf_op jit(solution)/shard_map/ppermute | solution.py:23
  114.6 2.0 collective-permute-start.9
  116.5 1.3 collective-permute-start.10
  117.8 3.0 %collective-permute-start.11 = (f32[16,4,1,128]{3,0,2,1:T(8,128)S(1)}, f32[16,4,1,128]{3,0,2,1:T(8,128)S(1)}, u32[]{:S(2)}, u32[]{:S(2)}) collective-permute-start(f32[16,4,1,128]{3,0,2,1:T(8,128)S(1)} %get-tuple-element.189), channel_id=1, source_target_pairs={{0,1},{1,2},{2,3},{4,5},{5,6},{6,7},{8,9},{9,10},{10,11},{12,13},{... | collective-permute-start | bytes 98312 | tf_op jit(solution)/shard_map/ppermute | solution.py:22
  122.6 21.8 %while.25 = (s32[]{:T(128)}, f32[16,4096]{1,0:T(8,128)S(1)}, f32[64]{0:T(128)S(1)}, s32[64]{0:T(128)S(1)}, s32[64]{0:T(128)S(1)}, /*index=5*/s32[64]{0:T(128)S(1)}, s32[64]{0:T(128)S(1)}, s32[]{:T(128)}) while((s32[]{:T(128)}, f32[16,4096]{1,0:T(8,128)S(1)}, f32[64]{0:T(128)S(1)}, s32[64]{0:T(128)S(1)}, ...), condition=%wide.region_6.7_spmd.clone.clone, body=%wide.region_5.6_spmd.clone.clone.sunk | while | flops 101466112 | bytes 2885461 | solution.py:122
  122.6 1.1 fusion.153
  124.4 1.1 fusion.153
  126.3 1.1 fusion.153
  128.1 1.1 fusion.153
  129.9 1.1 fusion.153
  131.7 1.1 fusion.153
  133.5 1.1 fusion.153
  135.3 1.1 fusion.153
  137.1 1.1 fusion.153
  139.0 1.1 fusion.153
  140.8 1.1 fusion.153
  145.3 20.2 %all_to_all.31 = f32[16,32,2,128]{3,2,1,0:T(2,128)S(1)} all-to-all(f32[16,32,2,128]{3,2,1,0:T(2,128)S(1)} %copy.20), channel_id=1, replica_groups=mesh['field'=16,'gx'=4,'gy'=4] {'field'}, dimensions={0} | all-to-all | bytes 1048576 | tf_op jit(solution)/shard_map/all_to_all | solution.py:42
  166.5 4.9 %all-to-all-start.4 = ((f32[16,16,2,128]{3,2,1,0:T(2,128)}), f32[16,16,2,128]{3,2,1,0:T(2,128)S(1)}, u32[]{:S(2)}, u32[]{:S(2)}) async-start(f32[16,16,2,128]{3,2,1,0:T(2,128)} %broadcast_in_dim.10), calls=%async_computation.4 | async-start | bytes 524288 | tf_op jit(solution)/shard_map/all_to_all | solution.py:57
  172.2 11.1 %all-to-all-done.4 = f32[16,16,2,128]{3,2,1,0:T(2,128)S(1)} async-done(((f32[16,16,2,128]{3,2,1,0:T(2,128)}), f32[16,16,2,128]{3,2,1,0:T(2,128)S(1)}, u32[]{:S(2)}, u32[]{:S(2)}) %all-to-all-start.4) | async-done | bytes 262176 | tf_op jit(solution)/shard_map/all_to_all | solution.py:57
  183.9 4.5 %all-to-all-start.5 = ((f32[16,2,128]{2,1,0:T(2,128)}), f32[16,2,128]{2,1,0:T(2,128)S(1)}, u32[]{:S(2)}, u32[]{:S(2)}) async-start(f32[16,2,128]{2,1,0:T(2,128)} %broadcast_in_dim.12), calls=%async_computation.5 | async-start | bytes 32768 | tf_op jit(solution)/shard_map/all_to_all | solution.py:57
  188.5 9.9 %all-to-all-done.5 = f32[16,2,128]{2,1,0:T(2,128)S(1)} async-done(((f32[16,2,128]{2,1,0:T(2,128)}), f32[16,2,128]{2,1,0:T(2,128)S(1)}, u32[]{:S(2)}, u32[]{:S(2)}) %all-to-all-start.5) | async-done | bytes 16416 | tf_op jit(solution)/shard_map/all_to_all | solution.py:57
  (99 shorter events, 30.6 us)
Async XLA Ops:
  1.1 5.9 %copy-start = (f32[4,8,128]{2,1,0:T(8,128)S(1)}, f32[4,8,128]{2,1,0:T(8,128)}, u32[]{:S(2)}) copy-start(f32[4,8,128]{2,1,0:T(8,128)} %param.13) | copy-start | bytes 49156
  1.1 23.9 %collective-permute-start.1 = (f32[16,1,8,128]{3,0,2,1:T(8,128)S(1)}, f32[16,1,8,128]{3,0,2,1:T(8,128)S(1)}, u32[]{:S(2)}, u32[]{:S(2)}) collective-permute-start(f32[16,1,8,128]{3,0,2,1:T(8,128)S(1)} %get-tuple-element.195), channel_id=1, source_target_pairs={{4,0},{8,4},{12,8},{5,1},{9,5},{13,9},{6,2},{10,6},{14,10},{7,3},{... | collective-permute-start | bytes 196616 | tf_op jit(solution)/shard_map/ppermute | solution.py:23
  3.6 21.5 %collective-permute-start.3 = (f32[16,1,8,128]{3,0,2,1:T(8,128)S(1)}, f32[16,1,8,128]{3,0,2,1:T(8,128)S(1)}, u32[]{:S(2)}, u32[]{:S(2)}) collective-permute-start(f32[16,1,8,128]{3,0,2,1:T(8,128)S(1)} %get-tuple-element.196), channel_id=1, source_target_pairs={{0,4},{4,8},{8,12},{1,5},{5,9},{9,13},{2,6},{6,10},{10,14},{3,7},{... | collective-permute-start | bytes 196616 | tf_op jit(solution)/shard_map/ppermute | solution.py:22
  7.0 11.4 %collective-permute-start.2 = (f32[1,8,128]{2,1,0:T(8,128)S(1)}, f32[1,8,128]{2,1,0:T(8,128)S(1)}, u32[]{:S(2)}, u32[]{:S(2)}) collective-permute-start(f32[1,8,128]{2,1,0:T(8,128)S(1)} %get-tuple-element.217), channel_id=1, source_target_pairs={{0,4},{4,8},{8,12},{1,5},{5,9},{9,13},{2,6},{6,10},{10,14},{3,7},{... | collective-permute-start | bytes 12296 | tf_op jit(solution)/shard_map/ppermute | solution.py:22
  9.0 4.4 %collective-permute-start.4 = (f32[4,1,128]{2,1,0:T(1,128)S(1)}, f32[4,1,128]{2,1,0:T(1,128)S(1)}, u32[]{:S(2)}, u32[]{:S(2)}) collective-permute-start(f32[4,1,128]{2,1,0:T(1,128)S(1)} %get-tuple-element.215), channel_id=1, source_target_pairs={{1,0},{2,1},{3,2},{5,4},{6,5},{7,6},{9,8},{10,9},{11,10},{13,12},{... | collective-permute-start | bytes 6152 | tf_op jit(solution)/shard_map/ppermute | solution.py:23
  10.3 3.1 %copy-start.4 = (s32[64,4]{0,1:T(4,128)S(1)}, s32[64,4]{0,1:T(4,128)}, u32[]{:S(2)}) copy-start(s32[64,4]{0,1:T(4,128)} %param.17) | copy-start | bytes 3076
  10.3 4.4 %collective-permute-start.6 = (f32[4,1,128]{2,1,0:T(1,128)S(1)}, f32[4,1,128]{2,1,0:T(1,128)S(1)}, u32[]{:S(2)}, u32[]{:S(2)}) collective-permute-start(f32[4,1,128]{2,1,0:T(1,128)S(1)} %get-tuple-element.214), channel_id=1, source_target_pairs={{0,1},{1,2},{2,3},{4,5},{5,6},{6,7},{8,9},{9,10},{10,11},{12,13},{... | collective-permute-start | bytes 6152 | tf_op jit(solution)/shard_map/ppermute | solution.py:22
  13.4 11.7 %collective-permute-start.5 = (f32[16,4,1,128]{3,0,2,1:T(8,128)S(1)}, f32[16,4,1,128]{3,0,2,1:T(8,128)S(1)}, u32[]{:S(2)}, u32[]{:S(2)}) collective-permute-start(f32[16,4,1,128]{3,0,2,1:T(8,128)S(1)} %get-tuple-element.194), channel_id=1, source_target_pairs={{1,0},{2,1},{3,2},{5,4},{6,5},{7,6},{9,8},{10,9},{11,10},{13,12},{... | collective-permute-start | bytes 98312 | tf_op jit(solution)/shard_map/ppermute | solution.py:23
  14.7 10.3 %collective-permute-start.7 = (f32[16,4,1,128]{3,0,2,1:T(8,128)S(1)}, f32[16,4,1,128]{3,0,2,1:T(8,128)S(1)}, u32[]{:S(2)}, u32[]{:S(2)}) collective-permute-start(f32[16,4,1,128]{3,0,2,1:T(8,128)S(1)} %get-tuple-element.193), channel_id=1, source_target_pairs={{0,1},{1,2},{2,3},{4,5},{5,6},{6,7},{8,9},{9,10},{10,11},{12,13},{... | collective-permute-start | bytes 98312 | tf_op jit(solution)/shard_map/ppermute | solution.py:22
  18.4 5.8 %copy-start.1 = (f32[2,3,1,4,8,128]{5,4,3,2,1,0:T(8,128)S(1)}, f32[2,3,1,4,8,128]{5,4,3,2,1,0:T(8,128)}, u32[]{:S(2)}) copy-start(f32[2,3,1,4,8,128]{5,4,3,2,1,0:T(8,128)} %param.14) | copy-start | bytes 294916
  18.5 5.6 %collective-permute-start = (f32[1,8,128]{2,1,0:T(8,128)S(1)}, f32[1,8,128]{2,1,0:T(8,128)S(1)}, u32[]{:S(2)}, u32[]{:S(2)}) collective-permute-start(f32[1,8,128]{2,1,0:T(8,128)S(1)} %get-tuple-element.216), channel_id=1, source_target_pairs={{4,0},{8,4},{12,8},{5,1},{9,5},{13,9},{6,2},{10,6},{14,10},{7,3},{... | collective-permute-start | bytes 12296 | tf_op jit(solution)/shard_map/ppermute | solution.py:23
  24.1 0.8 copy-start.3
  26.0 0.7 copy-start.2
  78.6 16.7 %all-to-all-start.1 = ((f32[16,16,2,128]{3,2,1,0:T(2,128)}), f32[16,16,2,128]{3,2,1,0:T(2,128)S(1)}, u32[]{:S(2)}, u32[]{:S(2)}) async-start(f32[16,16,2,128]{3,2,1,0:T(2,128)} %broadcast_in_dim.8), calls=%async_computation.1 | async-start | bytes 524288 | tf_op jit(solution)/shard_map/all_to_all | solution.py:57
  95.9 14.5 %all-to-all-start.2 = ((f32[16,2,128]{2,1,0:T(2,128)}), f32[16,2,128]{2,1,0:T(2,128)S(1)}, u32[]{:S(2)}, u32[]{:S(2)}) async-start(f32[16,2,128]{2,1,0:T(2,128)} %broadcast_in_dim.9), calls=%async_computation.2 | async-start | bytes 32768 | tf_op jit(solution)/shard_map/all_to_all | solution.py:57
  110.7 11.1 %collective-permute-start.8 = (f32[16,1,8,128]{3,0,2,1:T(8,128)S(1)}, f32[16,1,8,128]{3,0,2,1:T(8,128)S(1)}, u32[]{:S(2)}, u32[]{:S(2)}) collective-permute-start(f32[16,1,8,128]{3,0,2,1:T(8,128)S(1)} %get-tuple-element.191), channel_id=1, source_target_pairs={{4,0},{8,4},{12,8},{5,1},{9,5},{13,9},{6,2},{10,6},{14,10},{7,3},{... | collective-permute-start | bytes 196616 | tf_op jit(solution)/shard_map/ppermute | solution.py:23
  114.6 7.2 %collective-permute-start.9 = (f32[16,1,8,128]{3,0,2,1:T(8,128)S(1)}, f32[16,1,8,128]{3,0,2,1:T(8,128)S(1)}, u32[]{:S(2)}, u32[]{:S(2)}) collective-permute-start(f32[16,1,8,128]{3,0,2,1:T(8,128)S(1)} %get-tuple-element.192), channel_id=1, source_target_pairs={{0,4},{4,8},{8,12},{1,5},{5,9},{9,13},{2,6},{6,10},{10,14},{3,7},{... | collective-permute-start | bytes 196616 | tf_op jit(solution)/shard_map/ppermute | solution.py:22
  116.5 4.3 %collective-permute-start.10 = (f32[16,4,1,128]{3,0,2,1:T(8,128)S(1)}, f32[16,4,1,128]{3,0,2,1:T(8,128)S(1)}, u32[]{:S(2)}, u32[]{:S(2)}) collective-permute-start(f32[16,4,1,128]{3,0,2,1:T(8,128)S(1)} %get-tuple-element.190), channel_id=1, source_target_pairs={{1,0},{2,1},{3,2},{5,4},{6,5},{7,6},{9,8},{10,9},{11,10},{13,12},{... | collective-permute-start | bytes 98312 | tf_op jit(solution)/shard_map/ppermute | solution.py:23
  117.8 3.9 %collective-permute-start.11 = (f32[16,4,1,128]{3,0,2,1:T(8,128)S(1)}, f32[16,4,1,128]{3,0,2,1:T(8,128)S(1)}, u32[]{:S(2)}, u32[]{:S(2)}) collective-permute-start(f32[16,4,1,128]{3,0,2,1:T(8,128)S(1)} %get-tuple-element.189), channel_id=1, source_target_pairs={{0,1},{1,2},{2,3},{4,5},{5,6},{6,7},{8,9},{9,10},{10,11},{12,13},{... | collective-permute-start | bytes 98312 | tf_op jit(solution)/shard_map/ppermute | solution.py:22
  166.5 16.7 %all-to-all-start.4 = ((f32[16,16,2,128]{3,2,1,0:T(2,128)}), f32[16,16,2,128]{3,2,1,0:T(2,128)S(1)}, u32[]{:S(2)}, u32[]{:S(2)}) async-start(f32[16,16,2,128]{3,2,1,0:T(2,128)} %broadcast_in_dim.10), calls=%async_computation.4 | async-start | bytes 524288 | tf_op jit(solution)/shard_map/all_to_all | solution.py:57
  183.9 14.5 %all-to-all-start.5 = ((f32[16,2,128]{2,1,0:T(2,128)}), f32[16,2,128]{2,1,0:T(2,128)S(1)}, u32[]{:S(2)}, u32[]{:S(2)}) async-start(f32[16,2,128]{2,1,0:T(2,128)} %broadcast_in_dim.12), calls=%async_computation.5 | async-start | bytes 32768 | tf_op jit(solution)/shard_map/all_to_all | solution.py:57
where the time goes:
time: 202 us; the launch traced here: 199 us
  starting transfers between devices  50.3 us (25%)
  blocking collectives  48.5 us (24%)
  waiting for transfers between devices  44.4 us (22%)
  matrix products  42.8 us (21%)
  local copies, waits for them, and re-layouts  7.76 us (4%)
  other arithmetic  4.38 us (2%)
    all_to_all x2, blocking collectives, sum_at_owner(): lax.all_to_all(tiles, axis, split_axis=0, concat_axis=0, tiled=True)  48.5 us
    all_to_all x4, waiting for transfers between devices, copy_for_each(): return lax.all_to_all(copies, axis, split_axis=0, concat_axis=0, tiled=True)  42 us
    dot_general x24, matrix products, substep(): jnp.dot(react, logs, precision=highest)  26.3 us
    all_to_all x4, starting transfers between devices, copy_for_each(): return lax.all_to_all(copies, axis, split_axis=0, concat_axis=0, tiled=True)  18.9 us
    ppermute x6, starting transfers between devices, padded_2(): lax.ppermute(last, axis, up)  17.1 us
    dot_general x24, matrix products, substep(): return conc + chem_step * jnp.dot(net_t, flux, precision=highest)  16.5 us
    ppermute x6, starting transfers between devices, padded_2(): lax.ppermute(initial, axis, [(b, a) for a, b in up])  14.3 us
  transfers between devices with their start and end apart: 16, of which 6 were waited for; matrix products, arithmetic and copies ran while one was open for 1% of the time, Pallas kernels for 0%

commit v1 on v0

v1 whole, which is shorter than its diff:
```python
import functools

import jax
import jax.numpy as jnp
import numpy as np
from jax import lax
from jax.experimental import pallas as pl
from jax.experimental.pallas import tpu as pltpu
from jax.sharding import PartitionSpec as P

SUBSTEPS = 12
STEPS = 2
DT = 0.04
LOG2E = 1.4426950408889634
LN2 = 0.6931471805599453
f32 = jnp.float32
bf16 = jnp.bfloat16
MESH = pl.DeviceIdType.MESH


def split2(x):
    hi = x.astype(bf16)
    return hi, (x - hi.astype(f32)).astype(bf16)


def make_weights(reac, k_row, w1, w2):
    nr, ns = reac.shape[0], w2.shape[0]
    ids = lax.broadcasted_iota(jnp.int32, (nr, ns), 1)

    def one_hot(j):
        return (reac[:, j : j + 1] == ids).astype(f32)

    react = one_hot(0) + one_hot(1)
    net = one_hot(2) + one_hot(3) - react
    eye = lax.broadcasted_iota(jnp.int32, (nr, nr), 0) == lax.broadcasted_iota(
        jnp.int32, (nr, nr), 1
    )
    k_col = jnp.sum(jnp.where(eye, jnp.broadcast_to(k_row, (nr, nr)), 0.0), axis=1, keepdims=True)
    bias = jnp.log(k_col * (DT * LOG2E)) * LOG2E + 2.0 * float(np.log2(LN2))
    b0 = bias.astype(bf16).astype(f32)
    b1 = (bias - b0).astype(bf16).astype(f32)
    b2 = bias - b0 - b1
    cols = jnp.where(ids == 0, b0, jnp.where(ids == 1, b1, jnp.where(ids == 2, b2, 0.0)))
    w1[...] = jnp.concatenate([react, react, cols], axis=1).astype(bf16)
    net_t = net.T
    w2[...] = jnp.concatenate([net_t, net_t], axis=1).astype(bf16)


def log2_softplus(y):
    e = jnp.exp2(-jnp.abs(y))
    big = jnp.log(1.0 + e) * LOG2E
    small = e * (LOG2E - (0.5 * LOG2E) * e)
    s = jnp.maximum(y, 0.0) + jnp.where(e < 1e-4, small, big)
    return jnp.log(s) * LOG2E


def substep(y, w1, w2):
    hi, lo = split2(log2_softplus(y))
    ones = jnp.ones((16, y.shape[1]), bf16)
    x = jnp.concatenate([hi, lo, ones], axis=0)
    flux = jnp.exp2(jnp.dot(w1[...], x, preferred_element_type=f32))
    fh, fl = split2(flux)
    return y + jnp.dot(w2[...], jnp.concatenate([fh, fl], axis=0), preferred_element_type=f32)


def kernel(
    sizes,
    conc, vel, gam, wie, mix, rate, reac,
    out,
    pad, gxr, gyr, gys, gpad, coef, ybuf, w1, w2, share, energy,
    got_s, got_e, mean, decay,
    hs_send, hs_recv, g_send, g_recv, rs_send, rs_recv, ag_send, ag_recv,
):
    nf, ngx, ngy = sizes
    ns, lx, ly, lz = conc.shape[1:]
    per = lx * ly // nf
    me = lax.axis_index("field")
    gx = lax.axis_index("gx")
    gy = lax.axis_index("gy")
    has = {
        ("gx", 0): gx > 0,
        ("gx", 1): gx < ngx - 1,
        ("gy", 0): gy > 0,
        ("gy", 1): gy < ngy - 1,
    }
    at = {
        ("gx", 0): gx - 1,
        ("gx", 1): gx + 1,
        ("gy", 0): gy - 1,
        ("gy", 1): gy + 1,
    }
    sides = [("gx", 0), ("gx", 1), ("gy", 0), ("gy", 1)]

    barrier = pltpu.get_barrier_semaphore()
    for k in range(1, nf):
        pl.semaphore_signal(
            barrier, inc=1, device_id={"field": lax.rem(me + k, nf)}, device_id_type=MESH
        )
    for side in sides:

        @pl.when(has[side])
        def _(side=side):
            pl.semaphore_signal(barrier, inc=1, device_id={side[0]: at[side]}, device_id_type=MESH)

    neighbours = sum(has[s].astype(jnp.int32) for s in sides)

    for x in range(lx):
        pad[0, x + 1, 1 : ly + 1] = jnp.swapaxes(conc[0, :, x], 0, 1)
    for i in range(2):
        gys[i] = gam[:, (ly - 1) * i, :]
    zero_x = jnp.zeros((ly, ns, lz), f32)
    zero_y = jnp.zeros((lx, ns, lz), f32)
    for axis, i in sides:

        @pl.when(jnp.logical_not(has[axis, i]))
        def _(axis=axis, i=i):
            if axis == "gx":
                gxr[i] = jnp.zeros((ly, lz), f32)
                for step in range(STEPS):
                    pad[step, (lx + 1) * i, 1 : ly + 1] = zero_x
            else:
                gyr[i] = jnp.zeros((lx, lz), f32)
                for step in range(STEPS):
                    pad[step, 1 : lx + 1, (ly + 1) * i] = zero_y

    make_weights(reac[...], rate[...].reshape(1, -1), w1, w2)

    pl.semaphore_wait(barrier, neighbours + (nf - 1))

    def face_copy(step, n):
        axis, i = sides[n]
        if axis == "gx":
            src = pad.at[step, lx if i else 1, pl.ds(1, ly)]
            dst = pad.at[step, 0 if i else lx + 1, pl.ds(1, ly)]
        else:
            src = pad.at[step, pl.ds(1, lx), ly if i else 1]
            dst = pad.at[step, pl.ds(1, lx), 0 if i else ly + 1]
        m = n ^ 1
        return pltpu.make_async_remote_copy(
            src, dst, hs_send.at[step, n], hs_recv.at[step, m],
            device_id={axis: at[axis, i]}, device_id_type=MESH,
        )

    def face_arrival(step, n):
        axis, i = sides[n]
        if axis == "gx":
            dst = pad.at[step, (lx + 1) * i, pl.ds(1, ly)]
        else:
            dst = pad.at[step, pl.ds(1, lx), (ly + 1) * i]
        return pltpu.make_async_copy(dst, dst, hs_recv.at[step, n])

    def gamma_copy(n):
        axis, i = sides[n]
        if axis == "gx":
            src, dst = gam.at[(lx - 1) * i], gxr.at[1 - i]
        else:
            src, dst = gys.at[i], gyr.at[1 - i]
        return pltpu.make_async_remote_copy(
            src, dst, g_send.at[n], g_recv.at[n ^ 1],
            device_id={axis: at[axis, i]}, device_id_type=MESH,
        )

    def gamma_arrival(n):
        axis, i = sides[n]
        dst = gxr.at[i] if axis == "gx" else gyr.at[i]
        return pltpu.make_async_copy(dst, dst, g_recv.at[n])

    def for_sides(f):
        for n in range(4):
            pl.when(has[sides[n]])(functools.partial(f, n))

    def start_faces(step):
        for_sides(lambda n: face_copy(step, n).start())

    start_faces(0)
    for_sides(lambda n: gamma_copy(n).start())
    for_sides(lambda n: gamma_arrival(n).wait())

    lane = lax.broadcasted_iota(jnp.int32, (lx, ly, lz), 2)
    g = gam[...]
    gpad[0, 1 : ly + 1] = gxr[0]
    gpad[lx + 1, 1 : ly + 1] = gxr[1]
    gpad[1 : lx + 1, 1 : ly + 1] = g
    gpad[1 : lx + 1, 0] = gyr[0]
    gpad[1 : lx + 1, ly + 1] = gyr[1]
    first, last = lane == 0, lane == lz - 1
    up = [
        gpad[2 : lx + 2, 1 : ly + 1],
        gpad[1 : lx + 1, 2 : ly + 2],
        jnp.where(last, 0.0, pltpu.roll(g, lz - 1, 2)),
    ]
    down = [
        gpad[0:lx, 1 : ly + 1],
        gpad[1 : lx + 1, 0:ly],
        jnp.where(first, 0.0, pltpu.roll(g, 1, 2)),
    ]
    noise = jnp.sqrt(2.0 * g)
    centre = 1.0
    diff = []
    for d in range(3):
        a, b = 0.5 * (g + up[d]), 0.5 * (g + down[d])
        centre = centre - a - b
        diff.append((a, b))
    for step in range(STEPS):
        coef[step, 0] = centre
        for d in range(3):
            w = 0.5 * (noise * wie[step, d, 0] - vel[d])
            a, b = diff[d][0] + w, diff[d][1] - w
            if d == 2:
                a, b = jnp.where(last, 0.0, a), jnp.where(first, 0.0, b)
            coef[step, 1 + 2 * d] = a
            coef[step, 2 + 2 * d] = b

    for step in range(STEPS):
        for_sides(lambda n, step=step: face_arrival(step, n).wait())
        for x in range(lx):
            p = pad[step, x + 1, 1 : ly + 1]
            near = [
                p,
                pad[step, x + 2, 1 : ly + 1],
                pad[step, x, 1 : ly + 1],
                pad[step, x + 1, 2 : ly + 2],
                pad[step, x + 1, 0:ly],
                pltpu.roll(p, lz - 1, 2),
                pltpu.roll(p, 1, 2),
            ]
            total = 0.0
            for i, value in enumerate(near):
                total = total + value * coef[step, i, x][:, None, :]
            total = total * LOG2E
            for y in range(ly):
                ybuf[:, (x * ly + y) * lz : (x * ly + y + 1) * lz] = total[y]

        def chem(_, carry):
            ybuf[...] = substep(ybuf[...], w1, w2)
            return carry

        lax.fori_loop(0, SUBSTEPS, chem, 0)

        for c in range(lx * ly):
            r = ybuf[:, c * lz : (c + 1) * lz] * LN2
            share[step, c // per, c % per] = r
            energy[step, c // per, c % per : c % per + 1] = jnp.sum(r * r, axis=0, keepdims=True)

        def sum_copies(k, step=step):
            to = lax.rem(me + k, nf)
            slot = nf - 1 - k
            return [
                pltpu.make_async_remote_copy(
                    src.at[step, to], dst.at[step, slot],
                    rs_send.at[step, j, k], rs_recv.at[step, j, slot],
                    device_id={"field": to}, device_id_type=MESH,
                )
                for j, (src, dst) in enumerate(((share, got_s), (energy, got_e)))
            ]

        for k in range(1, nf):
            for copy in sum_copies(k):
                copy.start()
        total_s = share[step, me]
        total_e = energy[step, me]
        for k in range(1, nf):
            for copy in sum_copies(k):
                copy.wait_recv()
            total_s = total_s + got_s[step, nf - 1 - k]
            total_e = total_e + got_e[step, nf - 1 - k]
        m = total_s * (1.0 / nf)
        power = total_e * (1.0 / nf)
        spread = power - jnp.sum(m * m, axis=1)
        row = pl.multiple_of(lax.rem(me * per, ly), per)
        omega = mix[(me * per) // ly, pl.ds(row, per), :] * (1.0 + spread / (1.0 + power))
        mean[step, me] = m
        decay[step, me] = jnp.exp(-0.5 * omega)

        def mean_copies(k, step=step):
            to = lax.rem(me + k, nf)
            return [
                pltpu.make_async_remote_copy(
                    ref.at[step, me], ref.at[step, me],
                    ag_send.at[step, j, k], ag_recv.at[step, j, nf - k],
                    device_id={"field": to}, device_id_type=MESH,
                )
                for j, ref in enumerate((mean, decay))
            ]

        def mean_arrivals(k, step=step):
            owner = lax.rem(me + k, nf)
            return [
                pltpu.make_async_copy(
                    ref.at[step, owner], ref.at[step, owner], ag_recv.at[step, j, k]
                )
                for j, ref in enumerate((mean, decay))
            ]

        for k in range(1, nf):
            for copy in mean_copies(k):
                copy.start()
        for k in range(1, nf):
            for copy in mean_arrivals(k):
                copy.wait()

        for x in range(lx):
            planes = []
            for y in range(ly):
                c = x * ly + y
                m = mean[step, c // per, c % per]
                d = decay[step, c // per, c % per : c % per + 1]
                v = m + (share[step, c // per, c % per] - m) * d
                if step + 1 < STEPS:
                    pad[step + 1, x + 1, y + 1] = v
                else:
                    planes.append(v)
            if planes:
                out[0, :, x] = jnp.swapaxes(jnp.stack(planes), 0, 1)
        if step + 1 < STEPS:
            start_faces(step + 1)

        for k in range(1, nf):
            for copy in sum_copies(k) + mean_copies(k):
                copy.wait_send()

    for step in range(STEPS):
        for_sides(lambda n, step=step: face_copy(step, n).wait_send())
    for_sides(lambda n: gamma_copy(n).wait_send())


def on_device(nf, ngx, ngy, *args):
    conc = args[0]
    ns, lx, ly, lz = conc.shape[1:]
    nr = args[6].shape[0]
    per = lx * ly // nf
    vmem, dma = pltpu.VMEM, pltpu.SemaphoreType.DMA
    return pl.pallas_call(
        functools.partial(kernel, (nf, ngx, ngy)),
        out_shape=jax.ShapeDtypeStruct(conc.shape, f32),
        in_specs=[pl.BlockSpec(memory_space=pltpu.VMEM)] * 7,
        out_specs=pl.BlockSpec(memory_space=pltpu.VMEM),
        scratch_shapes=[
            vmem((STEPS, lx + 2, ly + 2, ns, lz), f32),
            vmem((2, ly, lz), f32),
            vmem((2, lx, lz), f32),
            vmem((2, lx, lz), f32),
            vmem((lx + 2, ly + 8, lz), f32),
            vmem((STEPS, 7, lx, ly, lz), f32),
            vmem((ns, lx * ly * lz), f32),
            vmem((nr, 2 * ns + 16), bf16),
            vmem((ns, 2 * nr), bf16),
            vmem((STEPS, nf, per, ns, lz), f32),
            vmem((STEPS, nf, per, lz), f32),
            vmem((STEPS, nf - 1, per, ns, lz), f32),
            vmem((STEPS, nf - 1, per, lz), f32),
            vmem((STEPS, nf, per, ns, lz), f32),
            vmem((STEPS, nf, per, lz), f32),
            dma((STEPS, 4)),
            dma((STEPS, 4)),
            dma((4,)),
            dma((4,)),
            dma((STEPS, 2, nf)),
            dma((STEPS, 2, nf)),
            dma((STEPS, 2, nf)),
            dma((STEPS, 2, nf)),
        ],
        compiler_params=pltpu.CompilerParams(collective_id=0, has_side_effects=True),
        name="combustor",
    )(*args)


def solution(mesh):
    nf, ngx, ngy = (mesh.shape[a] for a in ("field", "gx", "gy"))
    return jax.shard_map(
        functools.partial(on_device, nf, ngx, ngy),
        mesh=mesh,
        in_specs=(
            P("field", None, "gx", "gy", None),
            P(None, "gx", "gy", None),
            P("gx", "gy", None),
            P(None, None, "field", "gx", "gy", None),
            P("gx", "gy", None),
            P(),
            P(),
        ),
        out_specs=P("field", None, "gx", "gy", None),
        check_vma=False,
    )
```

time: 202 us -> 73.7 us (0.36); the launches traced: 199 us -> 73.6 us
  Pallas kernels: 0 us -> 70.5 us
  starting transfers between devices: 50.3 us -> 0 us
  blocking collectives: 48.5 us -> 0 us
  waiting for transfers between devices: 44.4 us -> 0 us
  matrix products: 42.8 us -> 0 us
  local copies, waits for them, and re-layouts: 7.76 us -> 3.06 us
  other arithmetic: 4.38 us -> 0 us
    pallas_call x0 -> x1, Pallas kernels: none -> 70.5 us  [on_device(): pl.pallas_call(functools.partial(kernel, (nf, ngx, ngy)), out_shape=jax.S...]
    all_to_all x2 -> x0, blocking collectives: 48.5 us -> none  [sum_at_owner(): lax.all_to_all(tiles, axis, split_axis=0, concat_axis=0, tiled=True)]
    dot_general x48 -> x0, matrix products: 42.8 us -> none  [the longest x24 26.3 us: substep(): jnp.dot(react, logs, precision=highest)]
    all_to_all x4 -> x0, waiting for transfers between devices: 42 us -> none  [copy_for_each(): return lax.all_to_all(copies, axis, split_axis=0, concat_axis=0, tiled=True)]
    ppermute x12 -> x0, starting transfers between devices: 31.3 us -> none  [the longest x6 17.1 us: padded_2(): lax.ppermute(last, axis, up)]
    all_to_all x4 -> x0, starting transfers between devices: 18.9 us -> none  [copy_for_each(): return lax.all_to_all(copies, axis, split_axis=0, concat_axis=0, tiled=True)]
    broadcast_in_dim x4 -> x0, local copies, waits for them, and re-layouts: 2.83 us -> none  [copy_for_each(): copies = jnp.broadcast_to(value, (lax.axis_size(axis), *value.shape))]
    ppermute x12 -> x0, waiting for transfers between devices: 2.4 us -> none  [the longest x6 1.57 us: padded_2(): lax.ppermute(initial, axis, [(b, a) for a, b in up])]
  transfers between devices with their start and end apart: 16 -> 0, of which waited for: 6 -> 0; matrix products, arithmetic and copies ran while one was open for 1% -> 0% of each run, Pallas kernels for 0% -> 0%
where the time goes in v1:
time: 73.7 us; the launch traced here: 73.6 us
  Pallas kernels  70.5 us (96%)
  local copies, waits for them, and re-layouts  3.06 us (4%)
    pallas_call x1, Pallas kernels, on_device(): pl.pallas_call(functools.partial(kernel, (nf, ngx, ngy)), out_shape=jax.S...  70.5 us
    unnamed x2, local copies, waits for them, and re-layouts  3.06 us

profile of v1, /device:TPU:4, one launch (start us, length us, event | category | flops | bytes accessed | tf_op | source)
XLA Modules:
  0.0 73.6 jit_solution(6932575174834806393)
XLA Ops:
  0.0 1.4 %copy.8.reac = s32[64,4]{1,0:T(8,128)} copy(s32[64,4]{0,1:T(4,128)} %param.13) | data formatting | bytes 2048 | tf_op args[6]
  1.4 70.5 %combustor.1 = f32[1,16,4,8,128]{4,3,2,1,0:T(8,128)} custom-call(f32[1,16,4,8,128]{4,3,2,1,0:T(8,128)} %conc.1, f32[3,4,8,128]{3,2,1,0:T(8,128)} %vel.1, f32[4,8,128]{2,1,0:T(8,128)} %gam.1, f32[2,3,1,4,8,128]{5,4,3,2,1,0:T(8,128)} %wie.1, f32[4,8,128]{2,1,0:T(8,128)} %mix.1, f32[64]{0:T(128)} %rate.1, s32[64,4]{1,0:T(8,128)} %copy.8.reac), custom_call_target="tpu_custom_call" | custom-call | tf_op jit(solution)/shard_map/combustor/pallas_call | solution.py:333
  71.9 1.7 %copy.10 = f32[1,16,4,8,128]{4,3,2,1,0:T(8,128)} copy(f32[1,16,4,8,128]{4,3,2,1,0:T(8,128)} %combustor.1) | data formatting | bytes 524288

commit v2 on v1

--- a/solution.py
+++ b/solution.py
@@ -11,6 +11,8 @@
 SUBSTEPS = 12
 STEPS = 2
 DT = 0.04
+TILE = 256
+UNROLL = 12
 LOG2E = 1.4426950408889634
 LN2 = 0.6931471805599453
 f32 = jnp.float32
@@ -24,14 +26,16 @@
 
 
 def make_weights(reac, k_row, w1, w2):
-    nr, ns = reac.shape[0], w2.shape[0]
+    nr, ns = reac.shape[1], w2.shape[0]
     ids = lax.broadcasted_iota(jnp.int32, (nr, ns), 1)
+    scalar = lax.broadcasted_iota(jnp.int32, (ns, nr), 0)
 
     def one_hot(j):
-        return (reac[:, j : j + 1] == ids).astype(f32)
-
-    react = one_hot(0) + one_hot(1)
-    net = one_hot(2) + one_hot(3) - react
+        return (reac[j : j + 1] == scalar).astype(f32)
+
+    react_t = one_hot(0) + one_hot(1)
+    net_t = one_hot(2) + one_hot(3) - react_t
+    react = react_t.T
     eye = lax.broadcasted_iota(jnp.int32, (nr, nr), 0) == lax.broadcasted_iota(
         jnp.int32, (nr, nr), 1
     )
@@ -42,7 +46,6 @@
     b2 = bias - b0 - b1
     cols = jnp.where(ids == 0, b0, jnp.where(ids == 1, b1, jnp.where(ids == 2, b2, 0.0)))
     w1[...] = jnp.concatenate([react, react, cols], axis=1).astype(bf16)
-    net_t = net.T
     w2[...] = jnp.concatenate([net_t, net_t], axis=1).astype(bf16)
 
 
@@ -58,9 +61,9 @@
     hi, lo = split2(log2_softplus(y))
     ones = jnp.ones((16, y.shape[1]), bf16)
     x = jnp.concatenate([hi, lo, ones], axis=0)
-    flux = jnp.exp2(jnp.dot(w1[...], x, preferred_element_type=f32))
+    flux = jnp.exp2(jnp.dot(w1, x, preferred_element_type=f32))
     fh, fl = split2(flux)
-    return y + jnp.dot(w2[...], jnp.concatenate([fh, fl], axis=0), preferred_element_type=f32)
+    return y + jnp.dot(w2, jnp.concatenate([fh, fl], axis=0), preferred_element_type=f32)
 
 
 def kernel(
@@ -91,11 +94,15 @@
     }
     sides = [("gx", 0), ("gx", 1), ("gy", 0), ("gy", 1)]
 
+    nz = nf // 2
+    offsets = [(a, b) for a in range(2) for b in range(nz) if a or b]
+    offsets.sort(key=lambda o: (-(2 * o[0] + min(o[1], nz - o[1])), o[1]))
+    back = [offsets.index((a, (nz - b) % nz)) for a, b in offsets]
+    high, low = me // nz, lax.rem(me, nz)
+    peers = [lax.rem(high + a, 2) * nz + lax.rem(low + b, nz) for a, b in offsets]
     barrier = pltpu.get_barrier_semaphore()
-    for k in range(1, nf):
-        pl.semaphore_signal(
-            barrier, inc=1, device_id={"field": lax.rem(me + k, nf)}, device_id_type=MESH
-        )
+    for to in peers:
+        pl.semaphore_signal(barrier, inc=1, device_id={"field": to}, device_id_type=MESH)
     for side in sides:
 
         @pl.when(has[side])
@@ -232,10 +239,15 @@
                 ybuf[:, (x * ly + y) * lz : (x * ly + y + 1) * lz] = total[y]
 
         def chem(_, carry):
-            ybuf[...] = substep(ybuf[...], w1, w2)
+            a, b = w1[...], w2[...]
+            ys = [ybuf[:, q * TILE : (q + 1) * TILE] for q in range(lx * ly * lz // TILE)]
+            for _ in range(UNROLL):
+                ys = [substep(y, a, b) for y in ys]
+            for q, y in enumerate(ys):
+                ybuf[:, q * TILE : (q + 1) * TILE] = y
             return carry
 
-        lax.fori_loop(0, SUBSTEPS, chem, 0)
+        lax.fori_loop(0, SUBSTEPS // UNROLL, chem, 0)
 
         for c in range(lx * ly):
             r = ybuf[:, c * lz : (c + 1) * lz] * LN2
@@ -243,8 +255,7 @@
             energy[step, c // per, c % per : c % per + 1] = jnp.sum(r * r, axis=0, keepdims=True)
 
         def sum_copies(k, step=step):
-            to = lax.rem(me + k, nf)
-            slot = nf - 1 - k
+            to, slot = peers[k], back[k]
             return [
                 pltpu.make_async_remote_copy(
                     src.at[step, to], dst.at[step, slot],
@@ -254,16 +265,16 @@
                 for j, (src, dst) in enumerate(((share, got_s), (energy, got_e)))
             ]
 
-        for k in range(1, nf):
+        for k in range(nf - 1):
             for copy in sum_copies(k):
                 copy.start()
         total_s = share[step, me]
         total_e = energy[step, me]
-        for k in range(1, nf):
+        for k in range(nf - 1):
             for copy in sum_copies(k):
                 copy.wait_recv()
-            total_s = total_s + got_s[step, nf - 1 - k]
-            total_e = total_e + got_e[step, nf - 1 - k]
+            total_s = total_s + got_s[step, back[k]]
+            total_e = total_e + got_e[step, back[k]]
         m = total_s * (1.0 / nf)
         power = total_e * (1.0 / nf)
         spread = power - jnp.sum(m * m, axis=1)
@@ -273,18 +284,18 @@
         decay[step, me] = jnp.exp(-0.5 * omega)
 
         def mean_copies(k, step=step):
-            to = lax.rem(me + k, nf)
+            to = peers[k]
             return [
                 pltpu.make_async_remote_copy(
                     ref.at[step, me], ref.at[step, me],
-                    ag_send.at[step, j, k], ag_recv.at[step, j, nf - k],
+                    ag_send.at[step, j, k], ag_recv.at[step, j, back[k]],
                     device_id={"field": to}, device_id_type=MESH,
                 )
                 for j, ref in enumerate((mean, decay))
             ]
 
         def mean_arrivals(k, step=step):
-            owner = lax.rem(me + k, nf)
+            owner = peers[k]
             return [
                 pltpu.make_async_copy(
                     ref.at[step, owner], ref.at[step, owner], ag_recv.at[step, j, k]
@@ -292,10 +303,10 @@
                 for j, ref in enumerate((mean, decay))
             ]
 
-        for k in range(1, nf):
+        for k in range(nf - 1):
             for copy in mean_copies(k):
                 copy.start()
-        for k in range(1, nf):
+        for k in range(nf - 1):
             for copy in mean_arrivals(k):
                 copy.wait()
 
@@ -315,7 +326,7 @@
         if step + 1 < STEPS:
             start_faces(step + 1)
 
-        for k in range(1, nf):
+        for k in range(nf - 1):
             for copy in sum_copies(k) + mean_copies(k):
                 copy.wait_send()
 
@@ -327,7 +338,8 @@
 def on_device(nf, ngx, ngy, *args):
     conc = args[0]
     ns, lx, ly, lz = conc.shape[1:]
-    nr = args[6].shape[0]
+    args = (*args[:6], args[6].T)
+    nr = args[6].shape[1]
     per = lx * ly // nf
     vmem, dma = pltpu.VMEM, pltpu.SemaphoreType.DMA
     return pl.pallas_call(

time: 73.7 us -> 62.4 us (0.85)
  Pallas kernels: 70.5 us -> 60.3 us
  local copies, waits for them, and re-layouts: 3.06 us -> 1.67 us
    pallas_call x1, Pallas kernels: 70.5 us -> 60.3 us  [on_device(): pl.pallas_call(functools.partial(kernel, (nf, ngx, ngy)), out_shape=jax.S...]
    unnamed x2 -> x1, local copies, waits for them, and re-layouts: 3.06 us -> 1.67 us
where the time goes in v2:
time: 62.4 us; the launch traced here: 61.9 us
  Pallas kernels  60.3 us (97%)
  local copies, waits for them, and re-layouts  1.67 us (3%)
    pallas_call x1, Pallas kernels, on_device(): pl.pallas_call(functools.partial(kernel, (nf, ngx, ngy)), out_shape=jax.S...  60.3 us
    unnamed x1, local copies, waits for them, and re-layouts  1.67 us

profile of v2, /device:TPU:4, one launch (start us, length us, event | category | flops | bytes accessed | tf_op | source)
XLA Modules:
  0.0 61.9 jit_solution(2153953838750826953)
XLA Ops:
  0.0 60.3 %combustor.1 = f32[1,16,4,8,128]{4,3,2,1,0:T(8,128)} custom-call(f32[1,16,4,8,128]{4,3,2,1,0:T(8,128)} %conc.1, f32[3,4,8,128]{3,2,1,0:T(8,128)} %vel.1, f32[4,8,128]{2,1,0:T(8,128)} %gam.1, f32[2,3,1,4,8,128]{5,4,3,2,1,0:T(8,128)} %wie.1, f32[4,8,128]{2,1,0:T(8,128)} %mix.1, f32[64]{0:T(128)} %rate.1, s32[4,64]{1,0:T(4,128)} %bitcast.1), custom_call_target="tpu_custom_call" | custom-call | tf_op jit(solution)/shard_map/combustor/pallas_call | solution.py:345
  60.3 1.7 %copy.9 = f32[1,16,4,8,128]{4,3,2,1,0:T(8,128)} copy(f32[1,16,4,8,128]{4,3,2,1,0:T(8,128)} %combustor.1) | data formatting | bytes 524288

commit v3 on v2

v3 whole, which is shorter than its diff:
```python
import functools

import jax
import jax.numpy as jnp
import numpy as np
from jax import lax
from jax.experimental import pallas as pl
from jax.experimental.pallas import tpu as pltpu
from jax.sharding import PartitionSpec as P

SUBSTEPS = 12
STEPS = 2
DT = 0.04
TILE = 256
AHEAD = (3, 10)
LOG2E = 1.4426950408889634
LN2 = 0.6931471805599453
f32 = jnp.float32
bf16 = jnp.bfloat16
MESH = pl.DeviceIdType.MESH


def split2(x):
    hi = x.astype(bf16)
    return hi, (x - hi.astype(f32)).astype(bf16)


def make_weights(reac, k_row, w1, w2):
    nr, ns = reac.shape[1], w2.shape[0]
    ids = lax.broadcasted_iota(jnp.int32, (nr, ns), 1)
    scalar = lax.broadcasted_iota(jnp.int32, (ns, nr), 0)

    def one_hot(j):
        return (reac[j : j + 1] == scalar).astype(f32)

    react_t = one_hot(0) + one_hot(1)
    net_t = one_hot(2) + one_hot(3) - react_t
    react = react_t.T
    eye = lax.broadcasted_iota(jnp.int32, (nr, nr), 0) == lax.broadcasted_iota(
        jnp.int32, (nr, nr), 1
    )
    k_col = jnp.sum(jnp.where(eye, jnp.broadcast_to(k_row, (nr, nr)), 0.0), axis=1, keepdims=True)
    bias = jnp.log(k_col * (DT * LOG2E)) * LOG2E + 2.0 * float(np.log2(LN2))
    b0 = bias.astype(bf16).astype(f32)
    b1 = (bias - b0).astype(bf16).astype(f32)
    b2 = bias - b0 - b1
    cols = jnp.where(ids == 0, b0, jnp.where(ids == 1, b1, jnp.where(ids == 2, b2, 0.0)))
    w1[...] = jnp.concatenate([react, react, cols], axis=1).astype(bf16)
    w2[...] = jnp.concatenate([net_t, net_t], axis=1).astype(bf16)


def log2_softplus(y):
    e = jnp.exp2(-jnp.abs(y))
    big = jnp.log(1.0 + e) * LOG2E
    small = e * (LOG2E - (0.5 * LOG2E) * e)
    s = jnp.maximum(y, 0.0) + jnp.where(e < 1e-4, small, big)
    return jnp.log(s) * LOG2E


def substep(y, w1, w2):
    hi, lo = split2(log2_softplus(y))
    ones = jnp.ones((16, y.shape[1]), bf16)
    x = jnp.concatenate([hi, lo, ones], axis=0)
    flux = jnp.exp2(jnp.dot(w1, x, preferred_element_type=f32))
    fh, fl = split2(flux)
    return y + jnp.dot(w2, jnp.concatenate([fh, fl], axis=0), preferred_element_type=f32)


def kernel(
    sizes,
    conc_h, vel_h, gam_h, wie_h, mix_h, rate_h, reac_h,
    out,
    conc, vel, gam, wie, mix, rate, reac, in_sem,
    pad, gxr, gyr, gys, gpad, coef, ybuf, w1, w2, share, got, mean,
    hs_send, hs_recv, g_send, g_recv, rs_send, rs_recv, ag_send, ag_recv,
):
    nf, ngx, ngy = sizes
    ns, lx, ly, lz = conc.shape[1:]
    planes = [list(range(1, lx - 1)), [0, lx - 1]]
    chunks = [[(x, y) for x in xs for y in range(ly)] for xs in planes]
    me = lax.axis_index("field")
    gx = lax.axis_index("gx")
    gy = lax.axis_index("gy")
    has = {
        ("gx", 0): gx > 0,
        ("gx", 1): gx < ngx - 1,
        ("gy", 0): gy > 0,
        ("gy", 1): gy < ngy - 1,
    }
    at = {
        ("gx", 0): gx - 1,
        ("gx", 1): gx + 1,
        ("gy", 0): gy - 1,
        ("gy", 1): gy + 1,
    }
    sides = [("gx", 0), ("gx", 1), ("gy", 0), ("gy", 1)]

    nz = nf // 2
    offsets = [(a, b) for a in range(2) for b in range(nz) if a or b]
    offsets.sort(key=lambda o: (-(2 * o[0] + min(o[1], nz - o[1])), o[1]))
    back = [offsets.index((a, (nz - b) % nz)) for a, b in offsets]
    high, low = me // nz, lax.rem(me, nz)
    peers = [lax.rem(high + a, 2) * nz + lax.rem(low + b, nz) for a, b in offsets]
    barrier = pltpu.get_barrier_semaphore()
    for to in peers:
        pl.semaphore_signal(barrier, inc=1, device_id={"field": to}, device_id_type=MESH)
    for side in sides:

        @pl.when(has[side])
        def _(side=side):
            pl.semaphore_signal(barrier, inc=1, device_id={side[0]: at[side]}, device_id_type=MESH)

    neighbours = sum(has[s].astype(jnp.int32) for s in sides)

    loads = [
        pltpu.make_async_copy(a, b, in_sem.at[i])
        for i, (a, b) in enumerate(
            (
                (conc_h, conc), (gam_h, gam), (reac_h, reac), (rate_h, rate),
                (wie_h, wie), (vel_h, vel), (mix_h, mix),
            )
        )
    ]
    for load in loads:
        load.start()
    for load in loads[:2]:
        load.wait()
    for x in range(lx):
        pad[0, x + 1, 1 : ly + 1] = jnp.swapaxes(conc[0, :, x], 0, 1)
    for i in range(2):
        gys[i] = gam[:, (ly - 1) * i, :]
    zero_x = jnp.zeros((ly, ns, lz), f32)
    zero_y = jnp.zeros((lx, ns, lz), f32)
    for axis, i in sides:

        @pl.when(jnp.logical_not(has[axis, i]))
        def _(axis=axis, i=i):
            if axis == "gx":
                gxr[i] = jnp.zeros((ly, lz), f32)
                for step in range(STEPS):
                    pad[step, (lx + 1) * i, 1 : ly + 1] = zero_x
            else:
                gyr[i] = jnp.zeros((lx, lz), f32)
                for step in range(STEPS):
                    pad[step, 1 : lx + 1, (ly + 1) * i] = zero_y

    for load in loads[2:]:
        load.wait()
    make_weights(reac[...], rate[...].reshape(1, -1), w1, w2)

    pl.semaphore_wait(barrier, neighbours + (nf - 1))

    pieces = [(n, p) for n in range(4) for p in ((0,) if n < 2 else (0, 1, 2))]
    of_chunk = [[q for q in pieces if q[1] == 2], [q for q in pieces if q[1] < 2]]

    def face(step, n, p, inside):
        axis, i = sides[n]
        if axis == "gx":
            x = (lx if i else 1) if inside else (lx + 1) * i
            return pad.at[step, x, pl.ds(1, ly)]
        y = (ly if i else 1) if inside else (ly + 1) * i
        if p == 2:
            return pad.at[step, pl.ds(2, lx - 2), y]
        return pad.at[step, lx if p else 1, y]

    def face_copy(step, n, p):
        axis, i = sides[n]
        return pltpu.make_async_remote_copy(
            face(step, n, p, True), face(step, n ^ 1, p, False),
            hs_send.at[step, n, p], hs_recv.at[step, n ^ 1, p],
            device_id={axis: at[axis, i]}, device_id_type=MESH,
        )

    def face_arrival(step, n, p):
        dst = face(step, n, p, False)
        return pltpu.make_async_copy(dst, dst, hs_recv.at[step, n, p])

    def gamma_copy(n):
        axis, i = sides[n]
        if axis == "gx":
            src, dst = gam.at[(lx - 1) * i], gxr.at[1 - i]
        else:
            src, dst = gys.at[i], gyr.at[1 - i]
        return pltpu.make_async_remote_copy(
            src, dst, g_send.at[n], g_recv.at[n ^ 1],
            device_id={axis: at[axis, i]}, device_id_type=MESH,
        )

    def gamma_arrival(n):
        axis, i = sides[n]
        dst = gxr.at[i] if axis == "gx" else gyr.at[i]
        return pltpu.make_async_copy(dst, dst, g_recv.at[n])

    def for_sides(f):
        for n in range(4):
            pl.when(has[sides[n]])(functools.partial(f, n))

    def for_pieces(step, chosen, f):
        for n in range(4):

            @pl.when(has[sides[n]])
            def _(n=n):
                for m, p in chosen:
                    if m == n:
                        f(step, n, p)

    def start_faces(step, chosen):
        for_pieces(step, chosen, lambda *q: face_copy(*q).start())

    for_sides(lambda n: gamma_copy(n).start())
    for chosen in of_chunk:
        start_faces(0, chosen)
    for_sides(lambda n: gamma_arrival(n).wait())

    lane = lax.broadcasted_iota(jnp.int32, (lx, ly, lz), 2)
    g = gam[...]
    gpad[0, 1 : ly + 1] = gxr[0]
    gpad[lx + 1, 1 : ly + 1] = gxr[1]
    gpad[1 : lx + 1, 1 : ly + 1] = g
    gpad[1 : lx + 1, 0] = gyr[0]
    gpad[1 : lx + 1, ly + 1] = gyr[1]
    first, last = lane == 0, lane == lz - 1
    up = [
        gpad[2 : lx + 2, 1 : ly + 1],
        gpad[1 : lx + 1, 2 : ly + 2],
        jnp.where(last, 0.0, pltpu.roll(g, lz - 1, 2)),
    ]
    down = [
        gpad[0:lx, 1 : ly + 1],
        gpad[1 : lx + 1, 0:ly],
        jnp.where(first, 0.0, pltpu.roll(g, 1, 2)),
    ]
    noise = jnp.sqrt(2.0 * g)
    centre = 1.0
    diff = []
    for d in range(3):
        a, b = 0.5 * (g + up[d]), 0.5 * (g + down[d])
        centre = centre - a - b
        diff.append((a, b))
    for step in range(STEPS):
        coef[step, 0] = centre
        for d in range(3):
            w = 0.5 * (noise * wie[step, d, 0] - vel[d])
            a, b = diff[d][0] + w, diff[d][1] - w
            if d == 2:
                a, b = jnp.where(last, 0.0, a), jnp.where(first, 0.0, b)
            coef[step, 1 + 2 * d] = a
            coef[step, 2 + 2 * d] = b

    for step in range(STEPS):
        def move(chunk, step=step):
            for x in planes[chunk]:
                p = pad[step, x + 1, 1 : ly + 1]
                near = [
                    p,
                    pad[step, x + 2, 1 : ly + 1],
                    pad[step, x, 1 : ly + 1],
                    pad[step, x + 1, 2 : ly + 2],
                    pad[step, x + 1, 0:ly],
                    pltpu.roll(p, lz - 1, 2),
                    pltpu.roll(p, 1, 2),
                ]
                total = 0.0
                for i, value in enumerate(near):
                    total = total + value * coef[step, i, x][:, None, :]
                total = total * LOG2E
                for y in range(ly):
                    ybuf[:, (x * ly + y) * lz : (x * ly + y + 1) * lz] = total[y]

        def react(which, count):
            a, b = w1[...], w2[...]
            starts = [
                i for c in which for x in planes[c] for i in range(x * ly * lz, (x + 1) * ly * lz, TILE)
            ]
            ys = [ybuf[:, i : i + TILE] for i in starts]
            for _ in range(count):
                ys = [substep(y, a, b) for y in ys]
            for i, y in zip(starts, ys):
                ybuf[:, i : i + TILE] = y

        def sum_copy(c, k, step=step):
            return pltpu.make_async_remote_copy(
                share.at[step, c, peers[k]], got.at[step, c, back[k]],
                rs_send.at[step, c, k], rs_recv.at[step, c, back[k]],
                device_id={"field": peers[k]}, device_id_type=MESH,
            )

        def mean_copy(c, k, step=step):
            return pltpu.make_async_remote_copy(
                mean.at[step, c, me], mean.at[step, c, me],
                ag_send.at[step, c, k], ag_recv.at[step, c, back[k]],
                device_id={"field": peers[k]}, device_id_type=MESH,
            )

        def publish(c, step=step):
            for o, (x, y) in enumerate(chunks[c]):
                at_cell = (x * ly + y) * lz
                r = ybuf[:, at_cell : at_cell + lz] * LN2
                share[step, c, o, 0:ns] = r
                share[step, c, o, ns : ns + 1] = jnp.sum(r * r, axis=0, keepdims=True)
            for k in range(nf - 1):
                sum_copy(c, k).start()

        for_pieces(step, of_chunk[0], lambda *q: face_arrival(*q).wait())
        move(0)
        react((0,), AHEAD[step])
        for_pieces(step, of_chunk[1], lambda *q: face_arrival(*q).wait())
        move(1)
        react((0, 1), SUBSTEPS - AHEAD[step])
        publish(0)
        react((1,), AHEAD[step])
        publish(1)

        for c in range(2):
            total = share[step, c, me]
            for k in range(nf - 1):
                sum_copy(c, k).wait_recv()
                total = total + got[step, c, back[k]]
            total = total * (1.0 / nf)
            m, power = total[0:ns], total[ns : ns + 1]
            spread = power - jnp.sum(m * m, axis=0, keepdims=True)
            x, y = me // ly, lax.rem(me, ly)
            x = x * (lx - 1) if c else x + 1
            omega = mix[x, pl.ds(y, 1), :] * (1.0 + spread / (1.0 + power))
            mean[step, c, me, 0:ns] = m
            mean[step, c, me, ns : ns + 1] = jnp.exp(-0.5 * omega)
            for k in range(nf - 1):
                mean_copy(c, k).start()

        for c, cells in enumerate(chunks):
            for k in range(nf - 1):
                pltpu.make_async_copy(
                    mean.at[step, c, peers[k]], mean.at[step, c, peers[k]], ag_recv.at[step, c, k]
                ).wait()
            for o, (x, y) in enumerate(cells):
                m = mean[step, c, o, 0:ns]
                v = m + (share[step, c, o, 0:ns] - m) * mean[step, c, o, ns : ns + 1]
                if step + 1 < STEPS:
                    pad[step + 1, x + 1, y + 1] = v
                else:
                    ybuf[:, (x * ly + y) * lz : (x * ly + y + 1) * lz] = v
            if step + 1 < STEPS:
                start_faces(step + 1, of_chunk[c])
        if step + 1 == STEPS:
            for x in range(lx):
                rows = [
                    ybuf[:, (x * ly + y) * lz : (x * ly + y + 1) * lz] for y in range(ly)
                ]
                out[0, :, x] = jnp.swapaxes(jnp.stack(rows), 0, 1)
        for c in range(2):
            for k in range(nf - 1):
                sum_copy(c, k).wait_send()
                mean_copy(c, k).wait_send()
    for step in range(STEPS):
        for_pieces(step, pieces, lambda *q: face_copy(*q).wait_send())
    for_sides(lambda n: gamma_copy(n).wait_send())


def on_device(nf, ngx, ngy, *args):
    conc = args[0]
    ns, lx, ly, lz = conc.shape[1:]
    args = (*args[:6], args[6].T)
    nr = args[6].shape[1]
    vmem, dma = pltpu.VMEM, pltpu.SemaphoreType.DMA
    return pl.pallas_call(
        functools.partial(kernel, (nf, ngx, ngy)),
        out_shape=jax.ShapeDtypeStruct(conc.shape, f32),
        in_specs=[pl.BlockSpec(memory_space=pltpu.HBM)] * 7,
        out_specs=pl.BlockSpec(memory_space=pltpu.VMEM),
        scratch_shapes=[
            *[vmem(a.shape, a.dtype) for a in args],
            dma((7,)),
            vmem((STEPS, lx + 2, ly + 2, ns, lz), f32),
            vmem((2, ly, lz), f32),
            vmem((2, lx, lz), f32),
            vmem((2, lx, lz), f32),
            vmem((lx + 2, ly + 8, lz), f32),
            vmem((STEPS, 7, lx, ly, lz), f32),
            vmem((ns, lx * ly * lz), f32),
            vmem((nr, 2 * ns + 16), bf16),
            vmem((ns, 2 * nr), bf16),
            vmem((STEPS, 2, nf, ns + 1, lz), f32),
            vmem((STEPS, 2, nf - 1, ns + 1, lz), f32),
            vmem((STEPS, 2, nf, ns + 1, lz), f32),
            dma((STEPS, 4, 3)),
            dma((STEPS, 4, 3)),
            dma((4,)),
            dma((4,)),
            dma((STEPS, 2, nf)),
            dma((STEPS, 2, nf)),
            dma((STEPS, 2, nf)),
            dma((STEPS, 2, nf)),
        ],
        compiler_params=pltpu.CompilerParams(collective_id=0, has_side_effects=True),
        name="combustor",
    )(*args)


def solution(mesh):
    nf, ngx, ngy = (mesh.shape[a] for a in ("field", "gx", "gy"))
    return jax.shard_map(
        functools.partial(on_device, nf, ngx, ngy),
        mesh=mesh,
        in_specs=(
            P("field", None, "gx", "gy", None),
            P(None, "gx", "gy", None),
            P("gx", "gy", None),
            P(None, None, "field", "gx", "gy", None),
            P("gx", "gy", None),
            P(),
            P(),
        ),
        out_specs=P("field", None, "gx", "gy", None),
        check_vma=False,
    )
```

time: 62.4 us -> 57.7 us (0.925)
  Pallas kernels: 60.3 us -> 55.9 us
    pallas_call x1, Pallas kernels: 60.3 us -> 55.9 us  [on_device(): pl.pallas_call(functools.partial(kernel, (nf, ngx, ngy)), out_shape=jax.S...]
where the time goes in v3:
time: 57.7 us; the launch traced here: 57.6 us
  Pallas kernels  55.9 us (97%)
  local copies, waits for them, and re-layouts  1.67 us (3%)
    pallas_call x1, Pallas kernels, on_device(): pl.pallas_call(functools.partial(kernel, (nf, ngx, ngy)), out_shape=jax.S...  55.9 us
    unnamed x1, local copies, waits for them, and re-layouts  1.67 us

profile of v3, /device:TPU:4, one launch (start us, length us, event | category | flops | bytes accessed | tf_op | source)
XLA Modules:
  0.0 57.6 jit_solution(1679815155371303991)
XLA Ops:
  0.0 55.9 %combustor.1 = f32[1,16,4,8,128]{4,3,2,1,0:T(8,128)} custom-call(f32[1,16,4,8,128]{4,3,2,1,0:T(8,128)} %conc_h.1, f32[3,4,8,128]{3,2,1,0:T(8,128)} %vel_h.1, f32[4,8,128]{2,1,0:T(8,128)} %gam_h.1, f32[2,3,1,4,8,128]{5,4,3,2,1,0:T(8,128)} %wie_h.1, f32[4,8,128]{2,1,0:T(8,128)} %mix_h.1, f32[64]{0:T(128)} %rate_h.1, s32[4,64]{1,0:T(4,128)} %bitcast.1), custom_call_target="tpu_custom_call" | custom-call | tf_op jit(solution)/shard_map/combustor/pallas_call | solution.py:365
  55.9 1.7 %copy.9 = f32[1,16,4,8,128]{4,3,2,1,0:T(8,128)} copy(f32[1,16,4,8,128]{4,3,2,1,0:T(8,128)} %combustor.1) | data formatting | bytes 524288

commit v4 on v3

--- a/solution.py
+++ b/solution.py
@@ -359,7 +359,7 @@
 def on_device(nf, ngx, ngy, *args):
     conc = args[0]
     ns, lx, ly, lz = conc.shape[1:]
-    args = (*args[:6], args[6].T)
+    args = tuple(pltpu.with_memory_space_constraint(a, pltpu.HBM) for a in (*args[:6], args[6].T))
     nr = args[6].shape[1]
     vmem, dma = pltpu.VMEM, pltpu.SemaphoreType.DMA
     return pl.pallas_call(
@@ -391,7 +391,7 @@
             dma((STEPS, 2, nf)),
             dma((STEPS, 2, nf)),
         ],
-        compiler_params=pltpu.CompilerParams(collective_id=0, has_side_effects=True),
+        compiler_params=pltpu.CompilerParams(collective_id=0, has_side_effects=True, vmem_limit_bytes=16777216),
         name="combustor",
     )(*args)
 

time: 57.7 us -> 55.9 us (0.969)
  local copies, waits for them, and re-layouts: 1.67 us -> 0.71 us
  Pallas kernels: 55.9 us -> 55.1 us
    unnamed x1, local copies, waits for them, and re-layouts: 1.67 us -> 0.71 us
    pallas_call x1, Pallas kernels: 55.9 us -> 55.1 us  [on_device(): pl.pallas_call(functools.partial(kernel, (nf, ngx, ngy)), out_shape=jax.S...]
where the time goes in v4:
time: 55.9 us; the launch traced here: 55.8 us
  Pallas kernels  55.1 us (99%)
  local copies, waits for them, and re-layouts  0.71 us (1%)
    pallas_call x1, Pallas kernels, on_device(): pl.pallas_call(functools.partial(kernel, (nf, ngx, ngy)), out_shape=jax.S...  55.1 us

profile of v4, /device:TPU:4, one launch (start us, length us, event | category | flops | bytes accessed | tf_op | source)
XLA Modules:
  0.0 55.8 jit_solution(8381039151111215178)
XLA Ops:
  0.0 55.1 %combustor.1 = f32[1,16,4,8,128]{4,3,2,1,0:T(8,128)S(1)} custom-call(f32[1,16,4,8,128]{4,3,2,1,0:T(8,128)} %conc_h.1, f32[3,4,8,128]{3,2,1,0:T(8,128)} %vel_h.1, f32[4,8,128]{2,1,0:T(8,128)} %gam_h.1, f32[2,3,1,4,8,128]{5,4,3,2,1,0:T(8,128)} %wie_h.1, f32[4,8,128]{2,1,0:T(8,128)} %mix_h.1, f32[64]{0:T(128)} %rate_h.1, s32[4,64]{1,0:T(4,128)} %bitcast.1), custom_call_target="tpu_custom_call" | custom-call | tf_op jit(solution)/shard_map/combustor/pallas_call | solution.py:365
  55.1 0.7 %copy.9 = f32[1,16,4,8,128]{4,3,2,1,0:T(8,128)} copy(f32[1,16,4,8,128]{4,3,2,1,0:T(8,128)S(1)} %combustor.1) | data formatting | bytes 524288

commit v5 on v4

--- a/solution.py
+++ b/solution.py
@@ -40,20 +40,19 @@
         jnp.int32, (nr, nr), 1
     )
     k_col = jnp.sum(jnp.where(eye, jnp.broadcast_to(k_row, (nr, nr)), 0.0), axis=1, keepdims=True)
-    bias = jnp.log(k_col * (DT * LOG2E)) * LOG2E + 2.0 * float(np.log2(LN2))
+    bias = jnp.log(k_col * (DT * LOG2E)) * LOG2E
     b0 = bias.astype(bf16).astype(f32)
     b1 = (bias - b0).astype(bf16).astype(f32)
     b2 = bias - b0 - b1
     cols = jnp.where(ids == 0, b0, jnp.where(ids == 1, b1, jnp.where(ids == 2, b2, 0.0)))
     w1[...] = jnp.concatenate([react, react, cols], axis=1).astype(bf16)
-    w2[...] = jnp.concatenate([net_t, net_t], axis=1).astype(bf16)
+    twice = [net_t[:, i : i + 16] for i in range(0, nr, 16) for _ in range(2)]
+    w2[...] = jnp.concatenate(twice, axis=1).astype(bf16)
 
 
 def log2_softplus(y):
     e = jnp.exp2(-jnp.abs(y))
-    big = jnp.log(1.0 + e) * LOG2E
-    small = e * (LOG2E - (0.5 * LOG2E) * e)
-    s = jnp.maximum(y, 0.0) + jnp.where(e < 1e-4, small, big)
+    s = jnp.maximum(y * LN2, 0.0) + jnp.where(e < 1e-4, e * (1.0 - 0.5 * e), jnp.log(1.0 + e))
     return jnp.log(s) * LOG2E
 
 
@@ -62,8 +61,8 @@
     ones = jnp.ones((16, y.shape[1]), bf16)
     x = jnp.concatenate([hi, lo, ones], axis=0)
     flux = jnp.exp2(jnp.dot(w1, x, preferred_element_type=f32))
-    fh, fl = split2(flux)
-    return y + jnp.dot(w2, jnp.concatenate([fh, fl], axis=0), preferred_element_type=f32)
+    parts = [part for i in range(0, flux.shape[0], 16) for part in split2(flux[i : i + 16])]
+    return y + jnp.dot(w2, jnp.concatenate(parts, axis=0), preferred_element_type=f32)
 
 
 def kernel(
@@ -101,17 +100,6 @@
     back = [offsets.index((a, (nz - b) % nz)) for a, b in offsets]
     high, low = me // nz, lax.rem(me, nz)
     peers = [lax.rem(high + a, 2) * nz + lax.rem(low + b, nz) for a, b in offsets]
-    barrier = pltpu.get_barrier_semaphore()
-    for to in peers:
-        pl.semaphore_signal(barrier, inc=1, device_id={"field": to}, device_id_type=MESH)
-    for side in sides:
-
-        @pl.when(has[side])
-        def _(side=side):
-            pl.semaphore_signal(barrier, inc=1, device_id={side[0]: at[side]}, device_id_type=MESH)
-
-    neighbours = sum(has[s].astype(jnp.int32) for s in sides)
-
     loads = [
         pltpu.make_async_copy(a, b, in_sem.at[i])
         for i, (a, b) in enumerate(
@@ -123,12 +111,90 @@
     ]
     for load in loads:
         load.start()
+    barrier = pltpu.get_barrier_semaphore()
+    for to in peers:
+        pl.semaphore_signal(barrier, inc=1, device_id={"field": to}, device_id_type=MESH)
+
+    for side in sides:
+
+        @pl.when(has[side])
+        def _(side=side):
+            pl.semaphore_signal(barrier, inc=1, device_id={side[0]: at[side]}, device_id_type=MESH)
+
+    neighbours = sum(has[s].astype(jnp.int32) for s in sides)
+
     for load in loads[:2]:
         load.wait()
     for x in range(lx):
         pad[0, x + 1, 1 : ly + 1] = jnp.swapaxes(conc[0, :, x], 0, 1)
     for i in range(2):
         gys[i] = gam[:, (ly - 1) * i, :]
+    pl.semaphore_wait(barrier, neighbours + (nf - 1))
+
+    pieces = [(n, p) for n in range(4) for p in ((0,) if n < 2 else (0, 1, 2))]
+    of_chunk = [[q for q in pieces if q[1] == 2], [q for q in pieces if q[1] < 2]]
+
+    def face(step, n, p, inside):
+        axis, i = sides[n]
+        if axis == "gx":
+            x = (lx if i else 1) if inside else (lx + 1) * i
+            return pad.at[step, x, pl.ds(1, ly)]
+        y = (ly if i else 1) if inside else (ly + 1) * i
+        if p == 2:
+            return pad.at[step, pl.ds(2, lx - 2), y]
+        return pad.at[step, lx if p else 1, y]
+
+    def face_copy(step, n, p):
+        axis, i = sides[n]
+        return pltpu.make_async_remote_copy(
+            face(step, n, p, True), face(step, n ^ 1, p, False),
+            hs_send.at[step, n, p], hs_recv.at[step, n ^ 1, p],
+            device_id={axis: at[axis, i]}, device_id_type=MESH,
+        )
+
+    def face_arrival(step, n, p):
+        dst = face(step, n, p, False)
+        return pltpu.make_async_copy(dst, dst, hs_recv.at[step, n, p])
+
+    def gamma_copy(n):
+        axis, i = sides[n]
+        if axis == "gx":
+            src, dst = gam.at[(lx - 1) * i], gxr.at[1 - i]
+        else:
+            src, dst = gys.at[i], gyr.at[1 - i]
+        return pltpu.make_async_remote_copy(
+            src, dst, g_send.at[n], g_recv.at[n ^ 1],
+            device_id={axis: at[axis, i]}, device_id_type=MESH,
+        )
+
+    def gamma_arrival(n):
+        axis, i = sides[n]
+        dst = gxr.at[i] if axis == "gx" else gyr.at[i]
+        return pltpu.make_async_copy(dst, dst, g_recv.at[n])
+
+    def for_sides(f):
+        for n in range(4):
+            pl.when(has[sides[n]])(functools.partial(f, n))
+
+    def for_pieces(step, chosen, f):
+        for n in range(4):
+
+            @pl.when(has[sides[n]])
+            def _(n=n):
+                for m, p in chosen:
+                    if m == n:
+                        f(step, n, p)
+
+    def start_faces(step, chosen):
+        for_pieces(step, chosen, lambda *q: face_copy(*q).start())
+
+    for_sides(lambda n: gamma_copy(n).start())
+    for chosen in of_chunk:
+        start_faces(0, chosen)
+    for load in loads[2:]:
+        load.wait()
+    make_weights(reac[...], rate[...].reshape(1, -1), w1, w2)
+
     zero_x = jnp.zeros((ly, ns, lz), f32)
     zero_y = jnp.zeros((lx, ns, lz), f32)
     for axis, i in sides:
@@ -144,72 +210,6 @@
                 for step in range(STEPS):
                     pad[step, 1 : lx + 1, (ly + 1) * i] = zero_y
 
-    for load in loads[2:]:
-        load.wait()
-    make_weights(reac[...], rate[...].reshape(1, -1), w1, w2)
-
-    pl.semaphore_wait(barrier, neighbours + (nf - 1))
-
-    pieces = [(n, p) for n in range(4) for p in ((0,) if n < 2 else (0, 1, 2))]
-    of_chunk = [[q for q in pieces if q[1] == 2], [q for q in pieces if q[1] < 2]]
-
-    def face(step, n, p, inside):
-        axis, i = sides[n]
-        if axis == "gx":
-            x = (lx if i else 1) if inside else (lx + 1) * i
-            return pad.at[step, x, pl.ds(1, ly)]
-        y = (ly if i else 1) if inside else (ly + 1) * i
-        if p == 2:
-            return pad.at[step, pl.ds(2, lx - 2), y]
-        return pad.at[step, lx if p else 1, y]
-
-    def face_copy(step, n, p):
-        axis, i = sides[n]
-        return pltpu.make_async_remote_copy(
-            face(step, n, p, True), face(step, n ^ 1, p, False),
-            hs_send.at[step, n, p], hs_recv.at[step, n ^ 1, p],
-            device_id={axis: at[axis, i]}, device_id_type=MESH,
-        )
-
-    def face_arrival(step, n, p):
-        dst = face(step, n, p, False)
-        return pltpu.make_async_copy(dst, dst, hs_recv.at[step, n, p])
-
-    def gamma_copy(n):
-        axis, i = sides[n]
-        if axis == "gx":
-            src, dst = gam.at[(lx - 1) * i], gxr.at[1 - i]
-        else:
-            src, dst = gys.at[i], gyr.at[1 - i]
-        return pltpu.make_async_remote_copy(
-            src, dst, g_send.at[n], g_recv.at[n ^ 1],
-            device_id={axis: at[axis, i]}, device_id_type=MESH,
-        )
-
-    def gamma_arrival(n):
-        axis, i = sides[n]
-        dst = gxr.at[i] if axis == "gx" else gyr.at[i]
-        return pltpu.make_async_copy(dst, dst, g_recv.at[n])
-
-    def for_sides(f):
-        for n in range(4):
-            pl.when(has[sides[n]])(functools.partial(f, n))
-
-    def for_pieces(step, chosen, f):
-        for n in range(4):
-
-            @pl.when(has[sides[n]])
-            def _(n=n):
-                for m, p in chosen:
-                    if m == n:
-                        f(step, n, p)
-
-    def start_faces(step, chosen):
-        for_pieces(step, chosen, lambda *q: face_copy(*q).start())
-
-    for_sides(lambda n: gamma_copy(n).start())
-    for chosen in of_chunk:
-        start_faces(0, chosen)
     for_sides(lambda n: gamma_arrival(n).wait())
 
     lane = lax.broadcasted_iota(jnp.int32, (lx, ly, lz), 2)
@@ -313,7 +313,7 @@
 
         for c in range(2):
             total = share[step, c, me]
-            for k in range(nf - 1):
+            for k in reversed(range(nf - 1)):
                 sum_copy(c, k).wait_recv()
                 total = total + got[step, c, back[k]]
             total = total * (1.0 / nf)
@@ -328,7 +328,7 @@
                 mean_copy(c, k).start()
 
         for c, cells in enumerate(chunks):
-            for k in range(nf - 1):
+            for k in reversed(range(nf - 1)):
                 pltpu.make_async_copy(
                     mean.at[step, c, peers[k]], mean.at[step, c, peers[k]], ag_recv.at[step, c, k]
                 ).wait()

time: 55.9 us -> 56 us (level)
  no operation moved by 1% of the time
where the time goes in v5:
time: 56 us; the launch traced here: 55.8 us
  Pallas kernels  55.1 us (98%)
  local copies, waits for them, and re-layouts  0.71 us (1%)
    pallas_call x1, Pallas kernels, on_device(): pl.pallas_call(functools.partial(kernel, (nf, ngx, ngy)), out_shape=jax.S...  55.1 us

profile of v5, /device:TPU:4, one launch (start us, length us, event | category | flops | bytes accessed | tf_op | source)
XLA Modules:
  0.0 55.8 jit_solution(8177893815797579731)
XLA Ops:
  0.0 55.1 %combustor.1 = f32[1,16,4,8,128]{4,3,2,1,0:T(8,128)S(1)} custom-call(f32[1,16,4,8,128]{4,3,2,1,0:T(8,128)} %conc_h.1, f32[3,4,8,128]{3,2,1,0:T(8,128)} %vel_h.1, f32[4,8,128]{2,1,0:T(8,128)} %gam_h.1, f32[2,3,1,4,8,128]{5,4,3,2,1,0:T(8,128)} %wie_h.1, f32[4,8,128]{2,1,0:T(8,128)} %mix_h.1, f32[64]{0:T(128)} %rate_h.1, s32[4,64]{1,0:T(4,128)} %bitcast.1), custom_call_target="tpu_custom_call" | custom-call | tf_op jit(solution)/shard_map/combustor/pallas_call | solution.py:365
  55.1 0.7 %copy.9 = f32[1,16,4,8,128]{4,3,2,1,0:T(8,128)} copy(f32[1,16,4,8,128]{4,3,2,1,0:T(8,128)S(1)} %combustor.1) | data formatting | bytes 524288

commit v6 on v5

--- a/solution.py
+++ b/solution.py
@@ -12,7 +12,7 @@
 STEPS = 2
 DT = 0.04
 TILE = 256
-AHEAD = (3, 10)
+AHEAD = (6, 10)
 LOG2E = 1.4426950408889634
 LN2 = 0.6931471805599453
 f32 = jnp.float32
@@ -210,42 +210,51 @@
                 for step in range(STEPS):
                     pad[step, 1 : lx + 1, (ly + 1) * i] = zero_y
 
-    for_sides(lambda n: gamma_arrival(n).wait())
-
-    lane = lax.broadcasted_iota(jnp.int32, (lx, ly, lz), 2)
-    g = gam[...]
-    gpad[0, 1 : ly + 1] = gxr[0]
-    gpad[lx + 1, 1 : ly + 1] = gxr[1]
-    gpad[1 : lx + 1, 1 : ly + 1] = g
+    lane = lax.broadcasted_iota(jnp.int32, (ly, lz), 1)
+    first, last = lane == 0, lane == lz - 1
+
+    def coefficients(chunk):
+        for x in planes[chunk]:
+            g = gam[x]
+            up = [
+                gpad[x + 2, 1 : ly + 1],
+                gpad[x + 1, 2 : ly + 2],
+                jnp.where(last, 0.0, pltpu.roll(g, lz - 1, 1)),
+            ]
+            down = [
+                gpad[x, 1 : ly + 1],
+                gpad[x + 1, 0:ly],
+                jnp.where(first, 0.0, pltpu.roll(g, 1, 1)),
+            ]
+            noise = jnp.sqrt(2.0 * g)
+            centre = 1.0
+            diff = []
+            for d in range(3):
+                a, b = 0.5 * (g + up[d]), 0.5 * (g + down[d])
+                centre = centre - a - b
+                diff.append((a, b))
+            for step in range(STEPS):
+                coef[step, 0, x] = centre
+                for d in range(3):
+                    w = 0.5 * (noise * wie[step, d, 0, x] - vel[d, x])
+                    a, b = diff[d][0] + w, diff[d][1] - w
+                    if d == 2:
+                        a, b = jnp.where(last, 0.0, a), jnp.where(first, 0.0, b)
+                    coef[step, 1 + 2 * d, x] = a
+                    coef[step, 2 + 2 * d, x] = b
+
+    gpad[1 : lx + 1, 1 : ly + 1] = gam[...]
+    for n in (2, 3):
+        pl.when(has[sides[n]])(functools.partial(lambda n: gamma_arrival(n).wait(), n))
     gpad[1 : lx + 1, 0] = gyr[0]
     gpad[1 : lx + 1, ly + 1] = gyr[1]
-    first, last = lane == 0, lane == lz - 1
-    up = [
-        gpad[2 : lx + 2, 1 : ly + 1],
-        gpad[1 : lx + 1, 2 : ly + 2],
-        jnp.where(last, 0.0, pltpu.roll(g, lz - 1, 2)),
-    ]
-    down = [
-        gpad[0:lx, 1 : ly + 1],
-        gpad[1 : lx + 1, 0:ly],
-        jnp.where(first, 0.0, pltpu.roll(g, 1, 2)),
-    ]
-    noise = jnp.sqrt(2.0 * g)
-    centre = 1.0
-    diff = []
-    for d in range(3):
-        a, b = 0.5 * (g + up[d]), 0.5 * (g + down[d])
-        centre = centre - a - b
-        diff.append((a, b))
-    for step in range(STEPS):
-        coef[step, 0] = centre
-        for d in range(3):
-            w = 0.5 * (noise * wie[step, d, 0] - vel[d])
-            a, b = diff[d][0] + w, diff[d][1] - w
-            if d == 2:
-                a, b = jnp.where(last, 0.0, a), jnp.where(first, 0.0, b)
-            coef[step, 1 + 2 * d] = a
-            coef[step, 2 + 2 * d] = b
+    coefficients(0)
+    def outer_coefficients():
+        for n in (0, 1):
+            pl.when(has[sides[n]])(functools.partial(lambda n: gamma_arrival(n).wait(), n))
+        gpad[0, 1 : ly + 1] = gxr[0]
+        gpad[lx + 1, 1 : ly + 1] = gxr[1]
+        coefficients(1)
 
     for step in range(STEPS):
         def move(chunk, step=step):
@@ -304,6 +313,8 @@
         for_pieces(step, of_chunk[0], lambda *q: face_arrival(*q).wait())
         move(0)
         react((0,), AHEAD[step])
+        if step == 0:
+            outer_coefficients()
         for_pieces(step, of_chunk[1], lambda *q: face_arrival(*q).wait())
         move(1)
         react((0, 1), SUBSTEPS - AHEAD[step])

time: 56 us -> 55.1 us (0.984)
  Pallas kernels: 55.1 us -> 54.1 us
    pallas_call x1, Pallas kernels: 55.1 us -> 54.1 us  [on_device(): pl.pallas_call(functools.partial(kernel, (nf, ngx, ngy)), out_shape=jax.S...]
where the time goes in v6:
time: 55.1 us; the launch traced here: 54.9 us
  Pallas kernels  54.1 us (98%)
  local copies, waits for them, and re-layouts  0.71 us (1%)
    pallas_call x1, Pallas kernels, on_device(): pl.pallas_call(functools.partial(kernel, (nf, ngx, ngy)), out_shape=jax.S...  54.1 us

profile of v6, /device:TPU:4, one launch (start us, length us, event | category | flops | bytes accessed | tf_op | source)
XLA Modules:
  0.0 54.9 jit_solution(17532876725211092305)
XLA Ops:
  0.0 54.1 %combustor.1 = f32[1,16,4,8,128]{4,3,2,1,0:T(8,128)S(1)} custom-call(f32[1,16,4,8,128]{4,3,2,1,0:T(8,128)} %conc_h.1, f32[3,4,8,128]{3,2,1,0:T(8,128)} %vel_h.1, f32[4,8,128]{2,1,0:T(8,128)} %gam_h.1, f32[2,3,1,4,8,128]{5,4,3,2,1,0:T(8,128)} %wie_h.1, f32[4,8,128]{2,1,0:T(8,128)} %mix_h.1, f32[64]{0:T(128)} %rate_h.1, s32[4,64]{1,0:T(4,128)} %bitcast.1), custom_call_target="tpu_custom_call" | custom-call | tf_op jit(solution)/shard_map/combustor/pallas_call | solution.py:376
  54.1 0.7 %copy.9 = f32[1,16,4,8,128]{4,3,2,1,0:T(8,128)} copy(f32[1,16,4,8,128]{4,3,2,1,0:T(8,128)S(1)} %combustor.1) | data formatting | bytes 524288
